TPU v7x, 256 devices: a whole 4x4x8 slice. The times are simulated.
256 devices in a mesh: fsdp: 8 (over x, y_hi), seq: 32 (over y_lo, z, core).
Axes of the slice: x: 4, y: 4 (y_hi: 2, y_lo: 2; y = y_hi * 2 + y_lo), z: 8, core: 2. Of those that a mesh axis runs over, the one named last changes fastest.
Arguments:
- q_next: bfloat16 [32768, 4096], P(('fsdp', 'seq')), may hold values from -9 to 9
- k_next: bfloat16 [32768, 1024], P(('fsdp', 'seq')), may hold values from -4 to 4
- v_next: bfloat16 [32768, 1024], P(('fsdp', 'seq')), may hold values from -6 to 6
- seg_next: int32 [8, 4096], P('fsdp'), may hold values from 0 to 15, never falling along the last dimension, each value on 1 to 512 neighbouring positions
- q_prev: bfloat16 [32768, 4096], P(('fsdp', 'seq')), may hold values from -9 to 9
- k_prev: bfloat16 [32768, 1024], P(('fsdp', 'seq')), may hold values from -4 to 4
- v_prev: bfloat16 [32768, 1024], P(('fsdp', 'seq')), may hold values from -6 to 6
- seg_prev: int32 [8, 4096], P('fsdp'), may hold values from 0 to 15, never falling along the last dimension, each value on 1 to 512 neighbouring positions
- upstream: bfloat16 [32768, 4096], P(('fsdp', 'seq')), may hold values from -6 to 6
- flags: int32 [8, 4096], P('fsdp', 'seq'), may hold values from 0 to 1
Outputs:
- attn_next: bfloat16 [32768, 4096], P(('fsdp', 'seq'))
- grad_q: bfloat16 [32768, 4096], P(('fsdp', 'seq'))
- grad_k: bfloat16 [32768, 1024], P(('fsdp', 'seq'))
- grad_v: bfloat16 [32768, 1024], P(('fsdp', 'seq'))
Inputs may be any that keep to these rules, and one draw needn't show every extreme that they name: `seg_next`: within each sequence the ids never fall and each id covers at most 512 consecutive positions; some id covers exactly 512. `seg_prev`: within each sequence the ids never fall and each id covers at most 512 consecutive positions; some id covers exactly 512.
All inputs are finite; a program needn't handle non-finite values.
Results may differ from a plain program's by a relative error of at most 0.0067.
Values may be sent and summed in bfloat16 or wider, within the bound.
A program may use at most 128 MiB of HBM per device.

v0:
```python
import functools

import jax
import jax.numpy as jnp
from jax import lax
from jax.sharding import Mesh
from jax.sharding import PartitionSpec as P

HEAD_DIM = 128
SEQ = ("seq_0", "seq_1", "seq_2")
FSDP = ("fsdp_0", "fsdp_1")
FSDP_SEQ = ("fsdp_0", "fsdp_1", "seq_0", "seq_1", "seq_2")


def passed_along(block, axis, distance):
    devices = range(lax.axis_size(axis))
    route = [(i - distance, i) for i in devices if i - distance in devices]
    return lax.ppermute(block, axis, route)


def by_axis(shard, axes):
    return functools.reduce(lax.psum, axes, shard)


def window_meta(seq_ids, rows_here, hop_total):
    width_all = (hop_total + 1) * rows_here
    first_row = lax.axis_index(SEQ) * rows_here
    padded = jnp.concatenate([jnp.full((hop_total * rows_here,), -1, jnp.int32), seq_ids])
    k_seg = lax.dynamic_slice_in_dim(padded, first_row, width_all)
    q_seg = lax.dynamic_slice_in_dim(seq_ids, first_row, rows_here)
    q_pos = first_row + jnp.arange(rows_here, dtype=jnp.int32)
    k_pos = first_row - hop_total * rows_here + jnp.arange(width_all, dtype=jnp.int32)
    keep_mask = (k_seg[None, :] == q_seg[:, None]) & (k_pos[None, :] <= q_pos[:, None])
    return keep_mask


def grouped_probs(grouped, k_window, keep_mask, scale_factor):
    scores = (
        jnp.einsum("qjgd,kjd->jgqk", grouped, k_window, preferred_element_type=jnp.float32)
        * scale_factor
    )
    scores = jnp.where(keep_mask[None, None], scores, -1e30)
    row_max = jnp.max(scores, axis=-1, keepdims=True)
    expo_vals = jnp.exp(scores - row_max)
    return expo_vals / jnp.sum(expo_vals, axis=-1, keepdims=True)


def forward_local(q_local, k_local, v_local, seq_ids, reach, scale_factor):
    rows_here = q_local.shape[0]
    head_dim = HEAD_DIM
    heads_all = q_local.shape[1] // head_dim
    kv_heads = k_local.shape[1] // head_dim
    group_size = heads_all // kv_heads
    hop_total = (reach + rows_here - 1) // rows_here
    key_list = [k_local]
    value_list = [v_local]
    for hop_count in range(1, hop_total + 1):
        far_keys, far_values = passed_along((k_local, v_local), SEQ, hop_count)
        key_list.insert(0, far_keys)
        value_list.insert(0, far_values)
    width_all = (hop_total + 1) * rows_here
    k_window = jnp.concatenate(key_list, axis=0).reshape(width_all, kv_heads, head_dim)
    v_window = jnp.concatenate(value_list, axis=0).reshape(width_all, kv_heads, head_dim)
    keep_mask = window_meta(seq_ids, rows_here, hop_total)
    grouped = q_local.reshape(rows_here, kv_heads, group_size, head_dim)
    soft_probs = grouped_probs(grouped, k_window, keep_mask, scale_factor)
    result = jnp.einsum(
        "jgqk,kjd->qjgd",
        soft_probs.astype(jnp.bfloat16),
        v_window,
        preferred_element_type=jnp.float32,
    )
    return result.astype(jnp.bfloat16).reshape(rows_here, heads_all * head_dim)


def backward_local(q_local, k_local, v_local, d_local, seq_ids, reach, scale_factor):
    rows_here = q_local.shape[0]
    head_dim = HEAD_DIM
    heads_all = q_local.shape[1] // head_dim
    kv_heads = k_local.shape[1] // head_dim
    group_size = heads_all // kv_heads
    hop_total = (reach + rows_here - 1) // rows_here
    key_list = [k_local]
    value_list = [v_local]
    for hop_count in range(1, hop_total + 1):
        far_keys, far_values = passed_along((k_local, v_local), SEQ, hop_count)
        key_list.insert(0, far_keys)
        value_list.insert(0, far_values)
    width_all = (hop_total + 1) * rows_here
    k_window = jnp.concatenate(key_list, axis=0).reshape(width_all, kv_heads, head_dim)
    v_window = jnp.concatenate(value_list, axis=0).reshape(width_all, kv_heads, head_dim)
    keep_mask = window_meta(seq_ids, rows_here, hop_total)
    grouped_q = q_local.reshape(rows_here, kv_heads, group_size, head_dim)
    grouped_d = d_local.reshape(rows_here, kv_heads, group_size, head_dim)
    soft_probs = grouped_probs(grouped_q, k_window, keep_mask, scale_factor)
    d_probs = jnp.einsum("qjgd,kjd->jgqk", grouped_d, v_window, preferred_element_type=jnp.float32)
    row_delta = jnp.sum(soft_probs * d_probs, axis=-1, keepdims=True)
    d_scores = (soft_probs * (d_probs - row_delta) * scale_factor).astype(jnp.bfloat16)
    q_grad = jnp.einsum("jgqk,kjd->qjgd", d_scores, k_window, preferred_element_type=jnp.float32)
    q_grad = q_grad.astype(jnp.bfloat16).reshape(rows_here, heads_all * head_dim)
    k_term = jnp.einsum(
        "jgqk,qjgd->kjd", d_scores, grouped_q, preferred_element_type=jnp.float32
    ).reshape(width_all, kv_heads * head_dim)
    v_term = jnp.einsum(
        "jgqk,qjgd->kjd",
        soft_probs.astype(jnp.bfloat16),
        grouped_d,
        preferred_element_type=jnp.float32,
    ).reshape(width_all, kv_heads * head_dim)
    k_total = k_term[hop_total * rows_here :]
    v_total = v_term[hop_total * rows_here :]
    for hop_count in range(1, hop_total + 1):
        start_row = (hop_total - hop_count) * rows_here
        back_keys, back_values = (
            passed_along(
                k_term[start_row : start_row + rows_here].astype(jnp.bfloat16), SEQ, -hop_count
            ).astype(jnp.float32),
            passed_along(
                v_term[start_row : start_row + rows_here].astype(jnp.bfloat16), SEQ, -hop_count
            ).astype(jnp.float32),
        )
        k_total = k_total + back_keys
        v_total = v_total + back_values
    return (q_grad, k_total.astype(jnp.bfloat16), v_total.astype(jnp.bfloat16))


def body(q_next, k_next, v_next, seg_next, q_prev, k_prev, v_prev, seg_prev, upstream, flags):
    rows_here = q_next.shape[0]
    head_dim = HEAD_DIM
    seq_size = lax.axis_size(SEQ)
    seq_len = rows_here * seq_size
    token_total = rows_here * lax.axis_size(FSDP) * seq_size
    reach = min(512, 4 * rows_here, seq_len // 2)
    scale_factor = head_dim ** (-0.5)
    next_ids = seg_next[0]
    prev_ids = seg_prev[0]
    flag_total = by_axis(jnp.sum(flags.astype(jnp.float32)), FSDP_SEQ)
    weight = flags.reshape(rows_here, 1).astype(jnp.float32) * (
        token_total / jnp.maximum(flag_total, 1.0)
    )
    cotangent = (upstream.astype(jnp.float32) * weight).astype(jnp.bfloat16)
    attn_next = forward_local(q_next, k_next, v_next, next_ids, reach, scale_factor)
    grad_q, grad_k, grad_v = backward_local(
        q_prev, k_prev, v_prev, cotangent, prev_ids, reach, scale_factor
    )
    return (attn_next, grad_q, grad_k, grad_v)


def solution(mesh):
    finer = Mesh(
        mesh.devices.reshape(4, 2, 2, 8, 2), ("fsdp_0", "fsdp_1", "seq_0", "seq_1", "seq_2")
    )
    in_specs = (
        P(FSDP_SEQ, None),
        P(FSDP_SEQ, None),
        P(FSDP_SEQ, None),
        P(FSDP, None),
        P(FSDP_SEQ, None),
        P(FSDP_SEQ, None),
        P(FSDP_SEQ, None),
        P(FSDP, None),
        P(FSDP_SEQ, None),
        P(FSDP, SEQ),
    )
    out_specs = (P(FSDP_SEQ, None), P(FSDP_SEQ, None), P(FSDP_SEQ, None), P(FSDP_SEQ, None))
    return jax.shard_map(body, mesh=finer, in_specs=in_specs, out_specs=out_specs, check_vma=False)
```

profile of v0, /device:TPU:9, one launch (start us, length us, event | category | flops | bytes accessed | tf_op | source)
XLA Modules:
  0.0 270.8 jit_solution(9223070849046800710)
XLA Ops:
  2.5 4.9 %collective-permute-start.8 = (bf16[128,1024]{0,1:T(8,128)(2,1)}, bf16[128,1024]{0,1:T(8,128)(2,1)}, u32[]{:S(2)}, u32[]{:S(2)}) collective-permute-start(bf16[128,1024]{0,1:T(8,128)(2,1)} %copy.46), channel_id=1, source_target_pairs={{0,4},{1,5},{2,6},{3,7},{4,8},{5,9},{6,10},{7,11},{8,12},{9,13},{1... | collective-permute-start | bytes 786440 | tf_op jit(solution)/shard_map/ppermute | solution.py:18
  7.4 7.0 %collective-permute-start.9 = (bf16[128,1024]{0,1:T(8,128)(2,1)}, bf16[128,1024]{0,1:T(8,128)(2,1)}, u32[]{:S(2)}, u32[]{:S(2)}) collective-permute-start(bf16[128,1024]{0,1:T(8,128)(2,1)} %copy.46), channel_id=1, source_target_pairs={{0,3},{1,4},{2,5},{3,6},{4,7},{5,8},{6,9},{7,10},{8,11},{9,12},{10... | collective-permute-start | bytes 786440 | tf_op jit(solution)/shard_map/ppermute | solution.py:18
  14.4 2.6 collective-permute-start.10
  20.1 3.1 %collective-permute-start.12 = (bf16[128,1024]{0,1:T(8,128)(2,1)S(1)}, bf16[128,1024]{0,1:T(8,128)(2,1)}, u32[]{:S(2)}, u32[]{:S(2)}) collective-permute-start(bf16[128,1024]{0,1:T(8,128)(2,1)S(1)} %copy.53), channel_id=1, source_target_pairs={{0,4},{1,5},{2,6},{3,7},{4,8},{5,9},{6,10},{7,11},{8,12},{9,13},{1... | collective-permute-start | bytes 786440 | tf_op jit(solution)/shard_map/ppermute | solution.py:18
  24.5 9.5 %psum.35 = f32[]{:T(128)} all-reduce(f32[]{:T(128)} %convert_reduce_fusion), channel_id=1, replica_groups=mesh['fsdp_0'=4,'fsdp_1'=2,'seq_0'=2,'seq_1'=8,'seq_2'=2] {'fsdp_0'}, use_global_device_ids=true, to_apply=%region_5.0 | all-reduce | flops 1 | bytes 8 | tf_op jit(solution)/shard_map/psum | solution.py:22
  34.0 6.3 %psum.36 = f32[]{:T(128)} all-reduce(f32[]{:T(128)} %psum.35), channel_id=1, replica_groups=mesh['fsdp_0'=4,'fsdp_1'=2,'seq_0'=2,'seq_1'=8,'seq_2'=2] {'fsdp_1'}, use_global_device_ids=true, to_apply=%region_6.7 | all-reduce | flops 1 | bytes 8 | tf_op jit(solution)/shard_map/psum | solution.py:22
  40.3 4.9 %psum.37 = f32[]{:T(128)} all-reduce(f32[]{:T(128)} %psum.36), channel_id=1, replica_groups=mesh['fsdp_0'=4,'fsdp_1'=2,'seq_0'=2,'seq_1'=8,'seq_2'=2] {'seq_0'}, use_global_device_ids=true, to_apply=%region_7.8 | all-reduce | flops 1 | bytes 8 | tf_op jit(solution)/shard_map/psum | solution.py:22
  45.2 12.6 %psum.38 = f32[]{:T(128)} all-reduce(f32[]{:T(128)} %psum.37), channel_id=1, replica_groups=mesh['fsdp_0'=4,'fsdp_1'=2,'seq_0'=2,'seq_1'=8,'seq_2'=2] {'seq_1'}, use_global_device_ids=true, to_apply=%region_8.9 | all-reduce | flops 1 | bytes 8 | tf_op jit(solution)/shard_map/psum | solution.py:22
  57.7 10.4 %psum.39 = f32[]{:T(128)} all-reduce(f32[]{:T(128)} %psum.38), channel_id=1, replica_groups=mesh['fsdp_0'=4,'fsdp_1'=2,'seq_0'=2,'seq_1'=8,'seq_2'=2] {'seq_2'}, use_global_device_ids=true, to_apply=%region_9.10 | all-reduce | flops 1 | bytes 8 | tf_op jit(solution)/shard_map/psum | solution.py:22
  85.4 4.1 %collective-permute-start.4 = (bf16[128,1024]{0,1:T(8,128)(2,1)S(1)}, bf16[128,1024]{0,1:T(8,128)(2,1)}, u32[]{:S(2)}, u32[]{:S(2)}) collective-permute-start(bf16[128,1024]{0,1:T(8,128)(2,1)S(1)} %copy.38), channel_id=1, source_target_pairs={{0,4},{1,5},{2,6},{3,7},{4,8},{5,9},{6,10},{7,11},{8,12},{9,13},{1... | collective-permute-start | bytes 786440 | tf_op jit(solution)/shard_map/ppermute | solution.py:18
  91.6 3.3 %collective-permute-start.5 = (bf16[128,1024]{0,1:T(8,128)(2,1)S(1)}, bf16[128,1024]{0,1:T(8,128)(2,1)}, u32[]{:S(2)}, u32[]{:S(2)}) collective-permute-start(bf16[128,1024]{0,1:T(8,128)(2,1)S(1)} %copy.38), channel_id=1, source_target_pairs={{0,3},{1,4},{2,5},{3,6},{4,7},{5,8},{6,9},{7,10},{8,11},{9,12},{10... | collective-permute-start | bytes 786440 | tf_op jit(solution)/shard_map/ppermute | solution.py:18
  102.8 5.5 %fusion.44 = f32[8,640,128,4]{2,1,3,0:T(8,128)} fusion(bf16[640,8,128,1]{0,2,3,1:T(8,128)(2,1)S(1)} %bitcast.130, bf16[128,8,4,128]{0,3,2,1:T(8,128)(2,1)S(1)} %bitcast.126), kind=kOutput, calls=%fused_computation.82 | convolution fusion | flops 671088640 | bytes 12845056 | tf_op jit(solution)/shard_map/qjgd,kjd->jgqk/dot_general | solution.py:96
  108.3 9.0 %fusion.41 = (f32[8,4,128]{2,1,0:T(4,128)S(1)}, f32[8,4,128,640]{2,3,1,0:T(8,128)}) fusion(pred[128,640]{0,1:T(8,128)(4,1)S(1)} %get-tuple-element.20, bf16[640,8,128,1]{0,2,3,1:T(8,128)(2,1)} %bitcast.145, bf16[128,8,4,128]{0,3,2,1:T(8,128)(2,1)} %bitcast.133), kind=kOutput, calls=%fused_computation.79 | convolution fusion | flops 681575040 | bytes 12943360 | tf_op jit(solution)/shard_map/sub | solution.py:44
  117.3 7.7 %fusion.43 = (bf16[640,8,128]{0,2,1:T(8,128)(2,1)}, f32[640,8,128]{0,2,1:T(8,128)}) fusion(bf16[128,8,4,128]{0,3,2,1:T(8,128)(2,1)S(1)} %bitcast.127, f32[8,4,128,640]{2,3,1,0:T(8,128)} %get-tuple-element.25, f32[8,4,128]{2,1,0:T(4,128)S(1)} %get-tuple-element.24), kind=kOutput, calls=%fused_computation.81 | convolution fusion | flops 676986880 | bytes 15482880 | tf_op jit(solution)/shard_map/jgqk,qjgd->kjd/dot_general | solution.py:104
  125.0 16.8 %fusion.42 = (bf16[640,8,128]{0,2,1:T(8,128)(2,1)S(1)}, f32[640,8,128]{0,2,1:T(8,128)}) fusion(bf16[128,8,4,128]{0,3,2,1:T(8,128)(2,1)} %bitcast.134, f32[8,640,128,4]{2,1,3,0:T(8,128)} %fusion.44, f32[8,4,128,640]{2,3,1,0:T(8,128)} %get-tuple-element.25, f32[8,4,128]{2,1,0:T(4,128)S(1)} %get-tuple-element.24), kind=kOutput, calls=%fused_computation.80 | convolution fusion | flops 690098816 | bytes 25968640 | tf_op jit(solution)/shard_map/jgqk,qjgd->kjd/dot_general | solution.py:101
  145.0 9.0 %collective-permute-start.1 = (bf16[128,1024]{1,0:T(8,128)(2,1)}, bf16[128,1024]{1,0:T(8,128)(2,1)}, u32[]{:S(2)}, u32[]{:S(2)}) collective-permute-start(bf16[128,1024]{1,0:T(8,128)(2,1)} %param.12), channel_id=1, source_target_pairs={{0,3},{1,4},{2,5},{3,6},{4,7},{5,8},{6,9},{7,10},{8,11},{9,12},{10... | collective-permute-start | bytes 786440 | tf_op jit(solution)/shard_map/ppermute | solution.py:18
  168.3 5.7 %collective-permute-start.21 = (bf16[128,1024]{1,0:T(8,128)(2,1)}, bf16[128,1024]{1,0:T(8,128)(2,1)}, u32[]{:S(2)}, u32[]{:S(2)}) collective-permute-start(bf16[128,1024]{1,0:T(8,128)(2,1)} %copy.72), channel_id=1, source_target_pairs={{2,0},{3,1},{4,2},{5,3},{6,4},{7,5},{8,6},{9,7},{10,8},{11,9},{12,... | collective-permute-start | bytes 786440 | tf_op jit(solution)/shard_map/ppermute | solution.py:18
  186.2 4.7 %collective-permute-start.22 = (bf16[128,1024]{1,0:T(8,128)(2,1)}, bf16[128,1024]{1,0:T(8,128)(2,1)S(1)}, u32[]{:S(2)}, u32[]{:S(2)}) collective-permute-start(bf16[128,1024]{1,0:T(8,128)(2,1)} %copy.73), channel_id=1, source_target_pairs={{3,0},{4,1},{5,2},{6,3},{7,4},{8,5},{9,6},{10,7},{11,8},{12,9},{13... | collective-permute-start | bytes 786440 | tf_op jit(solution)/shard_map/ppermute | solution.py:18
  205.0 2.9 %fusion.26 = f32[8,640,128,4]{2,1,3,0:T(8,128)S(1)} fusion(bf16[640,8,128,1]{0,2,3,1:T(8,128)(2,1)} %bitcast.131, bf16[128,8,4,128]{3,2,1,0:T(4,128)(2,1)S(1)} %reshape.200), kind=kOutput, calls=%fused_computation.33 | convolution fusion | flops 671088640 | bytes 12845056 | tf_op jit(solution)/shard_map/qjgd,kjd->jgqk/dot_general | solution.py:39
  207.9 6.9 %fusion.40 = (f32[8,4,128]{2,1,0:T(4,128)S(1)}, f32[8,4,128,640]{2,3,1,0:T(8,128)}) fusion(f32[8,640,128,4]{2,1,3,0:T(8,128)S(1)} %fusion.26, pred[128,640]{0,1:T(8,128)(4,1)S(1)} %get-tuple-element.21), kind=kOutput, calls=%fused_computation.78 | output fusion | flops 15729279 | bytes 21069824 | tf_op jit(solution)/shard_map/sub | solution.py:44
  214.8 5.4 %fusion.24 = bf16[8,128,4,128]{3,1,2,0:T(8,128)(2,1)S(1)} fusion(bf16[640,8,128,1]{0,2,3,1:T(8,128)(2,1)} %bitcast.132, f32[8,4,128,640]{2,3,1,0:T(8,128)} %get-tuple-element.23, f32[8,4,128]{2,1,0:T(4,128)S(1)} %get-tuple-element.22), kind=kOutput, calls=%fused_computation.31 | convolution fusion | flops 676855808 | bytes 12861440 | tf_op jit(solution)/shard_map/jgqk,kjd->qjgd/dot_general | solution.py:67
  220.2 16.1 %fusion.25 = bf16[8,128,4,128]{3,1,2,0:T(8,128)(2,1)} fusion(bf16[640,8,128,1]{0,2,3,1:T(8,128)(2,1)} %bitcast.146, f32[8,640,128,4]{2,1,3,0:T(8,128)} %fusion.44, f32[8,4,128,640]{2,3,1,0:T(8,128)} %get-tuple-element.25, f32[8,4,128]{2,1,0:T(4,128)S(1)} %get-tuple-element.24), kind=kOutput, calls=%fused_computation.32 | convolution fusion | flops 689967744 | bytes 23347200 | tf_op jit(solution)/shard_map/jgqk,kjd->qjgd/dot_general | solution.py:99
  249.5 13.5 %collective-permute-done.18 = bf16[128,1024]{1,0:T(8,128)(2,1)S(1)} collective-permute-done((bf16[128,1024]{1,0:T(8,128)(2,1)S(1)}, bf16[128,1024]{1,0:T(8,128)(2,1)S(1)}, u32[]{:S(2)}, u32[]{:S(2)}) %collective-permute-start.18) | collective-permute-done | bytes 262176 | tf_op jit(solution)/shard_map/ppermute | solution.py:18
  263.1 5.8 %collective-permute-done.19 = bf16[128,1024]{1,0:T(8,128)(2,1)S(1)} collective-permute-done((bf16[128,1024]{1,0:T(8,128)(2,1)S(1)}, bf16[128,1024]{1,0:T(8,128)(2,1)S(1)}, u32[]{:S(2)}, u32[]{:S(2)}) %collective-permute-start.19) | collective-permute-done | bytes 262176 | tf_op jit(solution)/shard_map/ppermute | solution.py:18
  (110 shorter events, 91.1 us)
Async XLA Ops:
  2.5 73.1 %collective-permute-start.8 = (bf16[128,1024]{0,1:T(8,128)(2,1)}, bf16[128,1024]{0,1:T(8,128)(2,1)}, u32[]{:S(2)}, u32[]{:S(2)}) collective-permute-start(bf16[128,1024]{0,1:T(8,128)(2,1)} %copy.46), channel_id=1, source_target_pairs={{0,4},{1,5},{2,6},{3,7},{4,8},{5,9},{6,10},{7,11},{8,12},{9,13},{1... | collective-permute-start | bytes 786440 | tf_op jit(solution)/shard_map/ppermute | solution.py:18
  7.4 71.3 %collective-permute-start.9 = (bf16[128,1024]{0,1:T(8,128)(2,1)}, bf16[128,1024]{0,1:T(8,128)(2,1)}, u32[]{:S(2)}, u32[]{:S(2)}) collective-permute-start(bf16[128,1024]{0,1:T(8,128)(2,1)} %copy.46), channel_id=1, source_target_pairs={{0,3},{1,4},{2,5},{3,6},{4,7},{5,8},{6,9},{7,10},{8,11},{9,12},{10... | collective-permute-start | bytes 786440 | tf_op jit(solution)/shard_map/ppermute | solution.py:18
  14.4 67.4 %collective-permute-start.10 = (bf16[128,1024]{0,1:T(8,128)(2,1)}, bf16[128,1024]{0,1:T(8,128)(2,1)}, u32[]{:S(2)}, u32[]{:S(2)}) collective-permute-start(bf16[128,1024]{0,1:T(8,128)(2,1)} %copy.46), channel_id=1, source_target_pairs={{0,2},{1,3},{2,4},{3,5},{4,6},{5,7},{6,8},{7,9},{8,10},{9,11},{10,... | collective-permute-start | bytes 786440 | tf_op jit(solution)/shard_map/ppermute | solution.py:18
  17.1 68.3 %collective-permute-start.11 = (bf16[128,1024]{0,1:T(8,128)(2,1)}, bf16[128,1024]{0,1:T(8,128)(2,1)}, u32[]{:S(2)}, u32[]{:S(2)}) collective-permute-start(bf16[128,1024]{0,1:T(8,128)(2,1)} %copy.46), channel_id=1, source_target_pairs={{0,1},{1,2},{2,3},{3,4},{4,5},{5,6},{6,7},{7,8},{8,9},{9,10},{10,1... | collective-permute-start | bytes 786440 | tf_op jit(solution)/shard_map/ppermute | solution.py:18
  20.1 71.5 %collective-permute-start.12 = (bf16[128,1024]{0,1:T(8,128)(2,1)S(1)}, bf16[128,1024]{0,1:T(8,128)(2,1)}, u32[]{:S(2)}, u32[]{:S(2)}) collective-permute-start(bf16[128,1024]{0,1:T(8,128)(2,1)S(1)} %copy.53), channel_id=1, source_target_pairs={{0,4},{1,5},{2,6},{3,7},{4,8},{5,9},{6,10},{7,11},{8,12},{9,13},{1... | collective-permute-start | bytes 786440 | tf_op jit(solution)/shard_map/ppermute | solution.py:18
  75.7 20.3 %collective-permute-start.13 = (bf16[128,1024]{0,1:T(8,128)(2,1)S(1)}, bf16[128,1024]{0,1:T(8,128)(2,1)S(1)}, u32[]{:S(2)}, u32[]{:S(2)}) collective-permute-start(bf16[128,1024]{0,1:T(8,128)(2,1)S(1)} %copy.53), channel_id=1, source_target_pairs={{0,3},{1,4},{2,5},{3,6},{4,7},{5,8},{6,9},{7,10},{8,11},{9,12},{10... | collective-permute-start | bytes 786440 | tf_op jit(solution)/shard_map/ppermute | solution.py:18
  78.8 19.4 %collective-permute-start.14 = (bf16[128,1024]{0,1:T(8,128)(2,1)S(1)}, bf16[128,1024]{0,1:T(8,128)(2,1)S(1)}, u32[]{:S(2)}, u32[]{:S(2)}) collective-permute-start(bf16[128,1024]{0,1:T(8,128)(2,1)S(1)} %copy.53), channel_id=1, source_target_pairs={{0,2},{1,3},{2,4},{3,5},{4,6},{5,7},{6,8},{7,9},{8,10},{9,11},{10,... | collective-permute-start | bytes 786440 | tf_op jit(solution)/shard_map/ppermute | solution.py:18
  81.9 18.7 %collective-permute-start.15 = (bf16[128,1024]{0,1:T(8,128)(2,1)S(1)}, bf16[128,1024]{0,1:T(8,128)(2,1)S(1)}, u32[]{:S(2)}, u32[]{:S(2)}) collective-permute-start(bf16[128,1024]{0,1:T(8,128)(2,1)S(1)} %copy.53), channel_id=1, source_target_pairs={{0,1},{1,2},{2,3},{3,4},{4,5},{5,6},{6,7},{7,8},{8,9},{9,10},{10,1... | collective-permute-start | bytes 786440 | tf_op jit(solution)/shard_map/ppermute | solution.py:18
  85.4 59.6 %collective-permute-start.4 = (bf16[128,1024]{0,1:T(8,128)(2,1)S(1)}, bf16[128,1024]{0,1:T(8,128)(2,1)}, u32[]{:S(2)}, u32[]{:S(2)}) collective-permute-start(bf16[128,1024]{0,1:T(8,128)(2,1)S(1)} %copy.38), channel_id=1, source_target_pairs={{0,4},{1,5},{2,6},{3,7},{4,8},{5,9},{6,10},{7,11},{8,12},{9,13},{1... | collective-permute-start | bytes 786440 | tf_op jit(solution)/shard_map/ppermute | solution.py:18
  91.6 63.5 %collective-permute-start.5 = (bf16[128,1024]{0,1:T(8,128)(2,1)S(1)}, bf16[128,1024]{0,1:T(8,128)(2,1)}, u32[]{:S(2)}, u32[]{:S(2)}) collective-permute-start(bf16[128,1024]{0,1:T(8,128)(2,1)S(1)} %copy.38), channel_id=1, source_target_pairs={{0,3},{1,4},{2,5},{3,6},{4,7},{5,8},{6,9},{7,10},{8,11},{9,12},{10... | collective-permute-start | bytes 786440 | tf_op jit(solution)/shard_map/ppermute | solution.py:18
  96.0 62.1 %collective-permute-start.6 = (bf16[128,1024]{0,1:T(8,128)(2,1)S(1)}, bf16[128,1024]{0,1:T(8,128)(2,1)}, u32[]{:S(2)}, u32[]{:S(2)}) collective-permute-start(bf16[128,1024]{0,1:T(8,128)(2,1)S(1)} %copy.38), channel_id=1, source_target_pairs={{0,2},{1,3},{2,4},{3,5},{4,6},{5,7},{6,8},{7,9},{8,10},{9,11},{10,... | collective-permute-start | bytes 786440 | tf_op jit(solution)/shard_map/ppermute | solution.py:18
  98.2 65.2 %collective-permute-start.7 = (bf16[128,1024]{0,1:T(8,128)(2,1)S(1)}, bf16[128,1024]{0,1:T(8,128)(2,1)}, u32[]{:S(2)}, u32[]{:S(2)}) collective-permute-start(bf16[128,1024]{0,1:T(8,128)(2,1)S(1)} %copy.38), channel_id=1, source_target_pairs={{0,1},{1,2},{2,3},{3,4},{4,5},{5,6},{6,7},{7,8},{8,9},{9,10},{10,1... | collective-permute-start | bytes 786440 | tf_op jit(solution)/shard_map/ppermute | solution.py:18
  100.5 67.8 %collective-permute-start = (bf16[128,1024]{1,0:T(8,128)(2,1)}, bf16[128,1024]{1,0:T(8,128)(2,1)}, u32[]{:S(2)}, u32[]{:S(2)}) collective-permute-start(bf16[128,1024]{1,0:T(8,128)(2,1)} %param.12), channel_id=1, source_target_pairs={{0,4},{1,5},{2,6},{3,7},{4,8},{5,9},{6,10},{7,11},{8,12},{9,13},{1... | collective-permute-start | bytes 786440 | tf_op jit(solution)/shard_map/ppermute | solution.py:18
  145.0 41.2 %collective-permute-start.1 = (bf16[128,1024]{1,0:T(8,128)(2,1)}, bf16[128,1024]{1,0:T(8,128)(2,1)}, u32[]{:S(2)}, u32[]{:S(2)}) collective-permute-start(bf16[128,1024]{1,0:T(8,128)(2,1)} %param.12), channel_id=1, source_target_pairs={{0,3},{1,4},{2,5},{3,6},{4,7},{5,8},{6,9},{7,10},{8,11},{9,12},{10... | collective-permute-start | bytes 786440 | tf_op jit(solution)/shard_map/ppermute | solution.py:18
  155.1 37.5 %collective-permute-start.2 = (bf16[128,1024]{1,0:T(8,128)(2,1)}, bf16[128,1024]{1,0:T(8,128)(2,1)}, u32[]{:S(2)}, u32[]{:S(2)}) collective-permute-start(bf16[128,1024]{1,0:T(8,128)(2,1)} %param.12), channel_id=1, source_target_pairs={{0,2},{1,3},{2,4},{3,5},{4,6},{5,7},{6,8},{7,9},{8,10},{9,11},{10,... | collective-permute-start | bytes 786440 | tf_op jit(solution)/shard_map/ppermute | solution.py:18
  158.0 38.7 %collective-permute-start.3 = (bf16[128,1024]{1,0:T(8,128)(2,1)}, bf16[128,1024]{1,0:T(8,128)(2,1)}, u32[]{:S(2)}, u32[]{:S(2)}) collective-permute-start(bf16[128,1024]{1,0:T(8,128)(2,1)} %param.12), channel_id=1, source_target_pairs={{0,1},{1,2},{2,3},{3,4},{4,5},{5,6},{6,7},{7,8},{8,9},{9,10},{10,1... | collective-permute-start | bytes 786440 | tf_op jit(solution)/shard_map/ppermute | solution.py:18
  163.3 76.6 %collective-permute-start.20 = (bf16[128,1024]{1,0:T(8,128)(2,1)}, bf16[128,1024]{1,0:T(8,128)(2,1)}, u32[]{:S(2)}, u32[]{:S(2)}) collective-permute-start(bf16[128,1024]{1,0:T(8,128)(2,1)} %copy.70), channel_id=1, source_target_pairs={{1,0},{2,1},{3,2},{4,3},{5,4},{6,5},{7,6},{8,7},{9,8},{10,9},{11,1... | collective-permute-start | bytes 786440 | tf_op jit(solution)/shard_map/ppermute | solution.py:18
  168.3 73.6 %collective-permute-start.21 = (bf16[128,1024]{1,0:T(8,128)(2,1)}, bf16[128,1024]{1,0:T(8,128)(2,1)}, u32[]{:S(2)}, u32[]{:S(2)}) collective-permute-start(bf16[128,1024]{1,0:T(8,128)(2,1)} %copy.72), channel_id=1, source_target_pairs={{2,0},{3,1},{4,2},{5,3},{6,4},{7,5},{8,6},{9,7},{10,8},{11,9},{12,... | collective-permute-start | bytes 786440 | tf_op jit(solution)/shard_map/ppermute | solution.py:18
  186.2 58.2 %collective-permute-start.22 = (bf16[128,1024]{1,0:T(8,128)(2,1)}, bf16[128,1024]{1,0:T(8,128)(2,1)S(1)}, u32[]{:S(2)}, u32[]{:S(2)}) collective-permute-start(bf16[128,1024]{1,0:T(8,128)(2,1)} %copy.73), channel_id=1, source_target_pairs={{3,0},{4,1},{5,2},{6,3},{7,4},{8,5},{9,6},{10,7},{11,8},{12,9},{13... | collective-permute-start | bytes 786440 | tf_op jit(solution)/shard_map/ppermute | solution.py:18
  192.6 53.8 %collective-permute-start.23 = (bf16[128,1024]{1,0:T(8,128)(2,1)}, bf16[128,1024]{1,0:T(8,128)(2,1)}, u32[]{:S(2)}, u32[]{:S(2)}) collective-permute-start(bf16[128,1024]{1,0:T(8,128)(2,1)} %copy.74), channel_id=1, source_target_pairs={{4,0},{5,1},{6,2},{7,3},{8,4},{9,5},{10,6},{11,7},{12,8},{13,9},{1... | collective-permute-start | bytes 786440 | tf_op jit(solution)/shard_map/ppermute | solution.py:18
  196.8 51.6 %collective-permute-start.16 = (bf16[128,1024]{1,0:T(8,128)(2,1)}, bf16[128,1024]{1,0:T(8,128)(2,1)}, u32[]{:S(2)}, u32[]{:S(2)}) collective-permute-start(bf16[128,1024]{1,0:T(8,128)(2,1)} %copy.63), channel_id=1, source_target_pairs={{1,0},{2,1},{3,2},{4,3},{5,4},{6,5},{7,6},{8,7},{9,8},{10,9},{11,1... | collective-permute-start | bytes 786440 | tf_op jit(solution)/shard_map/ppermute | solution.py:18
  239.9 9.6 %collective-permute-start.17 = (bf16[128,1024]{1,0:T(8,128)(2,1)S(1)}, bf16[128,1024]{1,0:T(8,128)(2,1)S(1)}, u32[]{:S(2)}, u32[]{:S(2)}) collective-permute-start(bf16[128,1024]{1,0:T(8,128)(2,1)S(1)} %copy-done.6), channel_id=1, source_target_pairs={{2,0},{3,1},{4,2},{5,3},{6,4},{7,5},{8,6},{9,7},{10,8},{11,9},{12,... | collective-permute-start | bytes 786440 | tf_op jit(solution)/shard_map/ppermute | solution.py:18
  241.9 21.1 %collective-permute-start.18 = (bf16[128,1024]{1,0:T(8,128)(2,1)S(1)}, bf16[128,1024]{1,0:T(8,128)(2,1)S(1)}, u32[]{:S(2)}, u32[]{:S(2)}) collective-permute-start(bf16[128,1024]{1,0:T(8,128)(2,1)S(1)} %copy-done.5), channel_id=1, source_target_pairs={{3,0},{4,1},{5,2},{6,3},{7,4},{8,5},{9,6},{10,7},{11,8},{12,9},{13... | collective-permute-start | bytes 786440 | tf_op jit(solution)/shard_map/ppermute | solution.py:18
  244.5 24.5 %collective-permute-start.19 = (bf16[128,1024]{1,0:T(8,128)(2,1)S(1)}, bf16[128,1024]{1,0:T(8,128)(2,1)S(1)}, u32[]{:S(2)}, u32[]{:S(2)}) collective-permute-start(bf16[128,1024]{1,0:T(8,128)(2,1)S(1)} %copy-done.4), channel_id=1, source_target_pairs={{4,0},{5,1},{6,2},{7,3},{8,4},{9,5},{10,6},{11,7},{12,8},{13,9},{1... | collective-permute-start | bytes 786440 | tf_op jit(solution)/shard_map/ppermute | solution.py:18
  (10 other events, 273.6 us)
where the time goes:
time: 274 us; the launch traced here: 271 us
  starting transfers between devices  77.2 us (28%)
  matrix products  63.4 us (23%)
  local copies, waits for them, and re-layouts  49.6 us (18%)
  blocking collectives  43.6 us (16%)
  waiting for transfers between devices  20.6 us (8%)
  other arithmetic  14.5 us (5%)
    ppermute x24, starting transfers between devices, passed_along(): return lax.ppermute(block, axis, route)  77.2 us
    psum x5, blocking collectives, by_axis(): return functools.reduce(lax.psum, axes, shard)  43.6 us
    unnamed x41, local copies, waits for them, and re-layouts  23.1 us
    ppermute x24, waiting for transfers between devices, passed_along(): return lax.ppermute(block, axis, route)  20.6 us
    dot_general x1, matrix products, backward_local(): jnp.einsum('jgqk,qjgd->kjd', d_scores, grouped_q, preferred_element_type=...  16.8 us
    dot_general x1, matrix products, backward_local(): jnp.einsum('jgqk,kjd->qjgd', d_scores, k_window, preferred_element_type=j...  16.1 us
    sub x1, matrix products, grouped_probs(): expo_vals = jnp.exp(scores - row_max)  8.96 us
    dot_general x1, matrix products, backward_local(): jnp.einsum('jgqk,qjgd->kjd', soft_probs.astype(jnp.bfloat16), grouped_d,...  7.71 us
  transfers between devices with their start and end apart: 24, of which 3 were waited for; matrix products, arithmetic and copies ran while one was open for 46% of the time, Pallas kernels for 0%

commit v1 on v0

v1 whole, which is shorter than its diff:
```python
import functools
import math

import jax
import jax.numpy as jnp
from jax import lax
from jax.experimental import pallas as pl
from jax.experimental.pallas import tpu as pltpu
from jax.sharding import PartitionSpec as P

HEAD_DIM = 128
GROUP = 4
BLOCKS = 5
AHEAD = 2
LAG = 4
MESH = pl.DeviceIdType.MESH
F32 = jnp.float32
BF16 = jnp.bfloat16


def dot(a, b, dims):
    return lax.dot_general(a, b, (dims, ((), ())), preferred_element_type=F32)


def column_of(row):
    return jnp.transpose(jnp.broadcast_to(row, (128, row.shape[1])))


def kernel(
    sizes,
    q_next, k_next, v_next, seg_next, q_prev, k_prev, v_prev, seg_prev, upstream, flags,
    attn_out, gq_out, gk_out, gv_out,
    own, near, far, side, side_grads, side_recv, grads, far_send, far_recv, near_send, near_recv,
    q_prev_v, up_v, q_next_v, attn_v, gq_v, gk_v, gv_v, dq_t, bias, count_send, count_recv,
    load_sem, array_sem, out_sem, send_sem, recv_sem, gsend_sem, grecv_sem, csend_sem, crecv_sem,
):
    kv_heads, n_fsdp, n_seq = sizes
    chunks = 2 * kv_heads
    width = GROUP * HEAD_DIM
    seq_at = lax.axis_index("seq")
    fsdp_at = lax.axis_index("fsdp")
    core = seq_at % 2
    ahead_at = (seq_at + 2) % n_seq
    behind_at = (seq_at + n_seq - 2) % n_seq
    side_at = seq_at + 1 - 2 * core
    scale = HEAD_DIM ** -0.5

    partners = []
    step = 1
    while step < n_seq:
        partners.append({"seq": seq_at + step - 2 * step * ((seq_at // step) % 2)})
        step *= 2
    step = 1
    while step < n_fsdp:
        partners.append({"fsdp": fsdp_at + step - 2 * step * ((fsdp_at // step) % 2)})
        step *= 2
    rounds = len(partners)

    def remote(src, dst, sems, at, device):
        return pltpu.make_async_remote_copy(
            src_ref=src, dst_ref=dst, send_sem=sems[0].at[at], recv_sem=sems[1].at[at],
            device_id=device, device_id_type=MESH,
        )

    links = (send_sem, recv_sem)
    glinks = (gsend_sem, grecv_sem)

    def own_ahead(t):
        return remote(own.at[t], near.at[t], links, (0, t), {"seq": ahead_at})

    def near_ahead(t):
        return remote(near.at[t], far.at[t], links, (1, t), {"seq": ahead_at})

    def own_side(t):
        return remote(own.at[t], side.at[0, t], links, (2, t), {"seq": side_at})

    def near_side(t):
        return remote(near.at[t], side.at[1, t], links, (3, t), {"seq": side_at})

    def far_side(t):
        return remote(far.at[t], side.at[2, t], links, (4, t), {"seq": side_at})

    def grads_side(t):
        return remote(side_grads.at[t], side_recv.at[t], glinks, (0, t), {"seq": side_at})

    def far_back(t):
        return remote(far_send.at[t], far_recv.at[t], glinks, (1, t), {"seq": behind_at})

    def near_back(t):
        return remote(near_send.at[t], near_recv.at[t], glinks, (2, t), {"seq": behind_at})

    def count_to(r):
        return remote(count_send.at[r], count_recv.at[r], (csend_sem, crecv_sem), r, partners[r])

    def load(t, which):
        k_from, v_from = (k_prev, v_prev) if t < kv_heads else (k_next, v_next)
        src = (k_from, v_from)[which]
        columns = slice((t % kv_heads) * HEAD_DIM, (t % kv_heads + 1) * HEAD_DIM)
        return pltpu.make_async_copy(src.at[:, columns], own.at[t, which], load_sem.at[t, which])

    def wait_load(t):
        for which, src in enumerate((k_prev, v_prev)):
            pltpu.make_async_copy(
                src.at[:, 0:HEAD_DIM], own.at[t, which], load_sem.at[t, which]
            ).wait()

    def columns_of(g, count=GROUP):
        return pl.ds(pl.multiple_of(g * (count * HEAD_DIM), HEAD_DIM), count * HEAD_DIM)

    def attn_copy(g):
        return pltpu.make_async_copy(
            attn_v.at[:, columns_of(g)], attn_out.at[:, columns_of(g)], out_sem.at[0, g]
        )

    def gq_copy(g):
        return pltpu.make_async_copy(
            gq_v.at[:, columns_of(g)], gq_out.at[:, columns_of(g)], out_sem.at[1, g]
        )

    def gkv_copy(which, g):
        src, dst = ((gk_v, gk_out), (gv_v, gv_out))[which]
        return pltpu.make_async_copy(
            src.at[:, columns_of(g, 1)], dst.at[:, columns_of(g, 1)], out_sem.at[2 + which, g]
        )

    for t in range(chunks):
        load(t, 0).start()
        load(t, 1).start()
    arrays = ((q_prev, q_prev_v), (upstream, up_v), (q_next, q_next_v))
    array_copies = [
        pltpu.make_async_copy(src, dst, array_sem.at[i]) for i, (src, dst) in enumerate(arrays)
    ]
    for copy in array_copies:
        copy.start()

    barrier = pltpu.get_barrier_semaphore()
    peers = [{"seq": ahead_at}, {"seq": behind_at}] + partners
    for peer in peers:
        pl.semaphore_signal(barrier, inc=1, device_id=peer, device_id_type=MESH)

    count_send[0] = jnp.broadcast_to(
        jnp.sum(flags[...].astype(F32), axis=1, keepdims=True), count_send.shape[1:]
    )
    pl.semaphore_wait(barrier, len(peers))

    for t in range(AHEAD):
        wait_load(t)
        own_ahead(t).start()
        own_side(t).start()

    rows_at = lax.broadcasted_iota(jnp.int32, (HEAD_DIM, HEAD_DIM), 0)
    lanes_at = lax.broadcasted_iota(jnp.int32, (HEAD_DIM, HEAD_DIM), 1)
    for m, seg in enumerate((seg_prev, seg_next)):
        def ids_at(index, seg=seg):
            return seg[:, pl.ds(pl.multiple_of(index * HEAD_DIM, HEAD_DIM), HEAD_DIM)].astype(F32)

        q_ids = ids_at(seq_at)
        for d in range(BLOCKS):
            k_ids = column_of(ids_at((seq_at + n_seq - d) % n_seq))
            keep = k_ids == q_ids
            if d == 0:
                keep = keep & (rows_at <= lanes_at)
                block_bias = jnp.where(keep, 0.0, -1e30)
            else:
                block_bias = jnp.where(keep, 0.0, -1e30)
                block_bias = jnp.where(seq_at >= d, block_bias, -1e30)
            bias[m, d * HEAD_DIM : (d + 1) * HEAD_DIM, :] = block_bias

    def window(w, which):
        return jnp.concatenate(
            [own[w, which], side[1 - core, w, which], near[w, which],
             side[2 - core, w, which], far[w, which]],
            axis=0,
        )

    def stacked(ref, g, first, count):
        return jnp.concatenate(
            [
                ref[:, pl.ds(pl.multiple_of(g * width + j * HEAD_DIM, HEAD_DIM), HEAD_DIM)]
                for j in range(first, first + count)
            ],
            axis=0,
        )

    def expo(k_all, q_part, m):
        pair = bias[m]
        scores = dot(k_all, q_part, ((1,), (1,))) + jnp.concatenate([pair, pair], axis=1)
        top = jnp.max(scores, axis=0, keepdims=True)
        values = jnp.exp2((scores - top) * (scale * math.log2(math.e)))
        return values, 1.0 / jnp.sum(values, axis=0, keepdims=True)

    def backward(w):
        k_all, v_all = window(w, 0), window(w, 1)
        k_turned = jnp.transpose(k_all)
        flag_row = flags[...].astype(F32)
        flag_pair = jnp.concatenate([flag_row, flag_row], axis=1)
        dk = dv = None
        for half in range(2):
            q_part = stacked(q_prev_v, w, 2 * half, 2)
            u_part = stacked(up_v, w, 2 * half, 2)
            values, inverse = expo(k_all, q_part, 0)
            d_probs = dot(v_all, u_part, ((1,), (1,)))
            row_delta = jnp.sum(values * d_probs, axis=0, keepdims=True) * inverse
            probs = values * (inverse * flag_pair)
            d_scores = (probs * (d_probs - row_delta)).astype(BF16)
            dq_t[w, :, half * 256 : (half + 1) * 256] = dot(k_turned, d_scores, ((1,), (0,)))
            dk_part = dot(d_scores, q_part, ((1,), (0,)))
            dv_part = dot(probs.astype(BF16), u_part, ((1,), (0,)))
            dk = dk_part if dk is None else dk + dk_part
            dv = dv_part if dv is None else dv + dv_part
        for which, total in enumerate((dk, dv)):
            for d in range(BLOCKS):
                block = total[d * HEAD_DIM : (d + 1) * HEAD_DIM]
                if d % 2:
                    side_grads[w, d // 2, which] = block.astype(BF16)
                else:
                    grads[w, d // 2, which] = block

    def forward(w):
        g = w - kv_heads
        k_all, v_turned = window(w, 0), jnp.transpose(window(w, 1))
        for half in range(2):
            values, inverse = expo(k_all, stacked(q_next_v, g, 2 * half, 2), 1)
            mixed = dot(v_turned, values.astype(BF16), ((1,), (0,))) * inverse
            for j in range(2):
                at = pl.multiple_of(g * width + (2 * half + j) * HEAD_DIM, HEAD_DIM)
                attn_v[:, pl.ds(at, HEAD_DIM)] = jnp.transpose(
                    mixed[:, j * HEAD_DIM : (j + 1) * HEAD_DIM]
                ).astype(BF16)

    def factor_row():
        total = count_send[rounds, 0:1, :]
        return (HEAD_DIM * n_fsdp * n_seq) / jnp.maximum(total, 1.0)

    def finish_q(g):
        gain = factor_row() * scale
        for j in range(GROUP):
            at = pl.multiple_of(g * width + j * HEAD_DIM, HEAD_DIM)
            turned = jnp.transpose(dq_t[g, :, j * HEAD_DIM : (j + 1) * HEAD_DIM])
            gq_v[:, pl.ds(at, HEAD_DIM)] = (turned * gain).astype(BF16)

    def take_side(w):
        for part in range(2):
            grads[w, core + part] = grads[w, core + part] + side_recv[w, part].astype(F32)
        far_send[w] = grads[w, 2].astype(BF16)

    def take_far(w):
        near_send[w] = (grads[w, 1] + far_recv[w].astype(F32)).astype(BF16)

    def take_near(w):
        total = grads[w, 0] + near_recv[w].astype(F32)
        gain = factor_row()
        gk_v[:, columns_of(w, 1)] = (total[0] * (gain * scale)).astype(BF16)
        gv_v[:, columns_of(w, 1)] = (total[1] * gain).astype(BF16)

    def during(t, first, count):
        return pl.when((t >= first) & (t < first + count))

    for copy in array_copies:
        copy.wait()

    def one_step(t, carry):
        @during(t, 0, chunks - AHEAD)
        def _():
            wait_load(t + AHEAD)
            own_ahead(t + AHEAD).start()
            own_side(t + AHEAD).start()

        @during(t, 0, chunks)
        def _():
            own_ahead(t).wait_recv()
            near_ahead(t).start()
            near_side(t).start()

        @during(t, LAG - 1, chunks)
        def _():
            near_ahead(t - LAG + 1).wait_recv()
            far_side(t - LAG + 1).start()

        @during(t, LAG + 1, kv_heads)
        def _():
            grads_side(t - LAG - 1).start()

        @during(t, LAG + 2, kv_heads)
        def _():
            grads_side(t - LAG - 2).wait_recv()
            take_side(t - LAG - 2)

        @during(t, LAG + 4, kv_heads)
        def _():
            far_back(t - LAG - 4).wait_recv()
            take_far(t - LAG - 4)

        for r in range(1, rounds + 1):
            @pl.when(t == r)
            def _(r=r):
                count_to(r - 1).wait_recv()
                count_send[r] = count_send[r - 1] + count_recv[r - 1]

        @during(t, LAG + 6, kv_heads)
        def _():
            near_back(t - LAG - 6).wait_recv()
            take_near(t - LAG - 6)
            gkv_copy(0, t - LAG - 6).start()
            gkv_copy(1, t - LAG - 6).start()

        @during(t, LAG, chunks)
        def _():
            w = t - LAG
            own_side(w).wait_recv()
            near_side(w).wait_recv()
            far_side(w).wait_recv()

        @during(t, LAG, kv_heads)
        def _():
            backward(t - LAG)

        @during(t, LAG + kv_heads, kv_heads)
        def _():
            forward(t - LAG)
            attn_copy(t - LAG - kv_heads).start()

        @during(t, LAG + kv_heads, kv_heads)
        def _():
            finish_q(t - LAG - kv_heads)
            gq_copy(t - LAG - kv_heads).start()

        @during(t, LAG + 2, kv_heads)
        def _():
            far_back(t - LAG - 2).start()

        @during(t, LAG + 4, kv_heads)
        def _():
            near_back(t - LAG - 4).start()

        for r in range(rounds):
            @pl.when(t == r)
            def _(r=r):
                count_to(r).start()

        return carry

    steps = max(chunks + LAG, kv_heads + LAG + 6, rounds + 1)
    lax.fori_loop(0, steps, one_step, 0)

    def drain(t, carry):
        own_ahead(t).wait_send()
        near_ahead(t).wait_send()
        own_side(t).wait_send()
        near_side(t).wait_send()
        far_side(t).wait_send()
        return carry

    lax.fori_loop(0, chunks, drain, 0)

    def drain_back(g, carry):
        grads_side(g).wait_send()
        far_back(g).wait_send()
        near_back(g).wait_send()
        attn_copy(g).wait()
        gq_copy(g).wait()
        gkv_copy(0, g).wait()
        gkv_copy(1, g).wait()
        return carry

    lax.fori_loop(0, kv_heads, drain_back, 0)
    for r in range(rounds):
        count_to(r).wait_send()


def body(n_fsdp, n_seq, *args):
    q, k = args[0], args[1]
    rows = q.shape[0]
    kv_heads = k.shape[1] // HEAD_DIM
    chunks = 2 * kv_heads
    width = q.shape[1]
    rounds = int(math.log2(n_fsdp * n_seq))
    tile = (2, HEAD_DIM, HEAD_DIM)
    anywhere = pl.BlockSpec(memory_space=pl.ANY)
    vmem = pl.BlockSpec(memory_space=pltpu.VMEM)
    dma = pltpu.SemaphoreType.DMA
    return pl.pallas_call(
        functools.partial(kernel, (kv_heads, n_fsdp, n_seq)),
        out_shape=(
            jax.ShapeDtypeStruct(q.shape, BF16),
            jax.ShapeDtypeStruct(q.shape, BF16),
            jax.ShapeDtypeStruct(k.shape, BF16),
            jax.ShapeDtypeStruct(k.shape, BF16),
        ),
        in_specs=[
            anywhere, anywhere, anywhere, vmem, anywhere, anywhere, anywhere, vmem, anywhere, vmem,
        ],
        out_specs=(anywhere,) * 4,
        scratch_shapes=[
            pltpu.VMEM((chunks,) + tile, BF16),
            pltpu.VMEM((chunks,) + tile, BF16),
            pltpu.VMEM((chunks,) + tile, BF16),
            pltpu.VMEM((3, chunks) + tile, BF16),
            pltpu.VMEM((kv_heads, 2) + tile, BF16),
            pltpu.VMEM((kv_heads, 2) + tile, BF16),
            pltpu.VMEM((kv_heads, 3) + tile, F32),
            pltpu.VMEM((kv_heads,) + tile, BF16),
            pltpu.VMEM((kv_heads,) + tile, BF16),
            pltpu.VMEM((kv_heads,) + tile, BF16),
            pltpu.VMEM((kv_heads,) + tile, BF16),
            pltpu.VMEM((rows, width), BF16),
            pltpu.VMEM((rows, width), BF16),
            pltpu.VMEM((rows, width), BF16),
            pltpu.VMEM((rows, width), BF16),
            pltpu.VMEM((rows, width), BF16),
            pltpu.VMEM(k.shape, BF16),
            pltpu.VMEM(k.shape, BF16),
            pltpu.VMEM((kv_heads, HEAD_DIM, GROUP * HEAD_DIM), F32),
            pltpu.VMEM((2, BLOCKS * HEAD_DIM, HEAD_DIM), F32),
            pltpu.VMEM((rounds + 1, 8, 128), F32),
            pltpu.VMEM((rounds, 8, 128), F32),
            dma((chunks, 2)),
            dma((3,)),
            dma((4, kv_heads)),
            dma((5, chunks)),
            dma((5, chunks)),
            dma((3, kv_heads)),
            dma((3, kv_heads)),
            dma((rounds,)),
            dma((rounds,)),
        ],
        compiler_params=pltpu.CompilerParams(
            collective_id=0, has_side_effects=True, vmem_limit_bytes=60 * 1024 * 1024
        ),
    )(*args)


def solution(mesh):
    both = P(("fsdp", "seq"), None)
    ids = P("fsdp", None)
    return jax.shard_map(
        functools.partial(body, mesh.shape["fsdp"], mesh.shape["seq"]),
        mesh=mesh,
        in_specs=(both, both, both, ids, both, both, both, ids, both, P("fsdp", "seq")),
        out_specs=(both,) * 4,
        check_vma=False,
    )
```

time: 274 us -> 88.8 us (0.32)
  the two profiles are of different devices: /device:TPU:9 before, /device:TPU:1 now
where the time goes in v1:
time: 88.8 us; the launch traced here: 88.6 us
  Pallas kernels  82.7 us (93%)
  local copies, waits for them, and re-layouts  5.22 us (6%)
    pallas_call x1, Pallas kernels, body(): pl.pallas_call(functools.partial(kernel, (kv_heads, n_fsdp, n_seq)), out_...  82.7 us
    unnamed x10, local copies, waits for them, and re-layouts  5.22 us

profile of v1, /device:TPU:1, one launch (start us, length us, event | category | flops | bytes accessed | tf_op | source)
XLA Modules:
  0.0 88.6 jit_solution(5957058293991570179)
XLA Ops:
  0.6 82.7 %shard_map.129 = (bf16[128,4096]{1,0:T(8,128)(2,1)}, bf16[128,4096]{1,0:T(8,128)(2,1)}, bf16[128,1024]{1,0:T(8,128)(2,1)}, bf16[128,1024]{1,0:T(8,128)(2,1)}) custom-call(bf16[128,4096]{1,0:T(8,128)(2,1)} %q_next.1, bf16[128,1024]{1,0:T(8,128)(2,1)} %k_next.1, bf16[128,1024]{1,0:T(8,128)(2,1)} %v_next.1, s32[1,4096]{1,0:T(1,128)} %seg_next.1, ...), custom_call_target="tpu_custom_call" | custom-call | tf_op jit(solution)/shard_map/pallas_call | solution.py:382
  83.3 0.0 copy-start
  83.4 2.4 %copy.18 = bf16[128,4096]{1,0:T(8,128)(2,1)} copy(bf16[128,4096]{1,0:T(8,128)(2,1)} %get-tuple-element.8) | data formatting | bytes 2097152
  85.7 0.0 copy-done
  85.7 0.0 copy-start.2
  85.7 1.0 %copy.19 = bf16[128,4096]{1,0:T(8,128)(2,1)} copy(bf16[128,4096]{1,0:T(8,128)(2,1)S(1)} %copy-done) | data formatting | bytes 2097152
  86.7 0.1 copy-done.2
  86.8 0.0 copy-start.1
  86.8 0.7 copy.20
  87.5 0.3 copy-done.1
  87.9 0.7 copy.21
Async XLA Ops:
  83.3 2.4 %copy-start = (bf16[128,4096]{1,0:T(8,128)(2,1)S(1)}, bf16[128,4096]{1,0:T(8,128)(2,1)}, u32[]{:S(2)}) copy-start(bf16[128,4096]{1,0:T(8,128)(2,1)} %get-tuple-element.9) | copy-start | bytes 3145732
  85.7 1.1 %copy-start.2 = (bf16[128,1024]{1,0:T(8,128)(2,1)S(1)}, bf16[128,1024]{1,0:T(8,128)(2,1)}, u32[]{:S(2)}) copy-start(bf16[128,1024]{1,0:T(8,128)(2,1)} %get-tuple-element.10) | copy-start | bytes 786436
  86.8 1.0 %copy-start.1 = (bf16[128,1024]{1,0:T(8,128)(2,1)S(1)}, bf16[128,1024]{1,0:T(8,128)(2,1)}, u32[]{:S(2)}) copy-start(bf16[128,1024]{1,0:T(8,128)(2,1)} %get-tuple-element.11) | copy-start | bytes 786436

commit v2 on v1

--- a/solution.py
+++ b/solution.py
@@ -12,6 +12,7 @@
 GROUP = 4
 BLOCKS = 5
 AHEAD = 2
+COUNT_STEPS = 5
 LAG = 4
 MESH = pl.DeviceIdType.MESH
 F32 = jnp.float32
@@ -29,12 +30,12 @@
 def kernel(
     sizes,
     q_next, k_next, v_next, seg_next, q_prev, k_prev, v_prev, seg_prev, upstream, flags,
-    attn_out, gq_out, gk_out, gv_out,
+    attn_v, gq_v, gk_v, gv_v,
     own, near, far, side, side_grads, side_recv, grads, far_send, far_recv, near_send, near_recv,
-    q_prev_v, up_v, q_next_v, attn_v, gq_v, gk_v, gv_v, dq_t, bias, count_send, count_recv,
-    load_sem, array_sem, out_sem, send_sem, recv_sem, gsend_sem, grecv_sem, csend_sem, crecv_sem,
+    q_prev_v, up_v, q_next_v, flags_v, seg_prev_v, seg_next_v, dq_t, bias, count_send, count_recv,
+    load_sem, array_sem, send_sem, recv_sem, gsend_sem, grecv_sem, csend_sem, crecv_sem,
 ):
-    kv_heads, n_fsdp, n_seq = sizes
+    kv_heads, n_fsdp, n_seq, plan = sizes
     chunks = 2 * kv_heads
     width = GROUP * HEAD_DIM
     seq_at = lax.axis_index("seq")
@@ -45,16 +46,15 @@
     side_at = seq_at + 1 - 2 * core
     scale = HEAD_DIM ** -0.5
 
-    partners = []
-    step = 1
-    while step < n_seq:
-        partners.append({"seq": seq_at + step - 2 * step * ((seq_at // step) % 2)})
-        step *= 2
-    step = 1
-    while step < n_fsdp:
-        partners.append({"fsdp": fsdp_at + step - 2 * step * ((fsdp_at // step) % 2)})
-        step *= 2
-    rounds = len(partners)
+    partners = [
+        [
+            {axis: at + ((at // stride % radix + j) % radix - at // stride % radix) * stride}
+            for j in range(1, radix)
+        ]
+        for axis, stride, radix in plan
+        for at in ((seq_at if axis == "seq" else fsdp_at),)
+    ]
+    rounds = len(plan)
 
     def remote(src, dst, sems, at, device):
         return pltpu.make_async_remote_copy(
@@ -89,8 +89,13 @@
     def near_back(t):
         return remote(near_send.at[t], near_recv.at[t], glinks, (2, t), {"seq": behind_at})
 
-    def count_to(r):
-        return remote(count_send.at[r], count_recv.at[r], (csend_sem, crecv_sem), r, partners[r])
+    def counts_to(r):
+        return [
+            remote(
+                count_send.at[r], count_recv.at[r, j], (csend_sem, crecv_sem), (r, j), partner
+            )
+            for j, partner in enumerate(partners[r])
+        ]
 
     def load(t, which):
         k_from, v_from = (k_prev, v_prev) if t < kv_heads else (k_next, v_next)
@@ -107,22 +112,17 @@
     def columns_of(g, count=GROUP):
         return pl.ds(pl.multiple_of(g * (count * HEAD_DIM), HEAD_DIM), count * HEAD_DIM)
 
-    def attn_copy(g):
-        return pltpu.make_async_copy(
-            attn_v.at[:, columns_of(g)], attn_out.at[:, columns_of(g)], out_sem.at[0, g]
-        )
-
-    def gq_copy(g):
-        return pltpu.make_async_copy(
-            gq_v.at[:, columns_of(g)], gq_out.at[:, columns_of(g)], out_sem.at[1, g]
-        )
-
-    def gkv_copy(which, g):
-        src, dst = ((gk_v, gk_out), (gv_v, gv_out))[which]
-        return pltpu.make_async_copy(
-            src.at[:, columns_of(g, 1)], dst.at[:, columns_of(g, 1)], out_sem.at[2 + which, g]
-        )
-
+    barrier = pltpu.get_barrier_semaphore()
+    peers = [{"seq": ahead_at}, {"seq": behind_at}] + sum(partners, [])
+    for peer in peers:
+        pl.semaphore_signal(barrier, inc=1, device_id=peer, device_id_type=MESH)
+
+    small = ((flags, flags_v), (seg_prev, seg_prev_v), (seg_next, seg_next_v))
+    small_copies = [
+        pltpu.make_async_copy(src, dst, array_sem.at[3 + i]) for i, (src, dst) in enumerate(small)
+    ]
+    for copy in small_copies:
+        copy.start()
     for t in range(chunks):
         load(t, 0).start()
         load(t, 1).start()
@@ -133,24 +133,15 @@
     for copy in array_copies:
         copy.start()
 
-    barrier = pltpu.get_barrier_semaphore()
-    peers = [{"seq": ahead_at}, {"seq": behind_at}] + partners
-    for peer in peers:
-        pl.semaphore_signal(barrier, inc=1, device_id=peer, device_id_type=MESH)
-
+    for copy in small_copies:
+        copy.wait()
     count_send[0] = jnp.broadcast_to(
-        jnp.sum(flags[...].astype(F32), axis=1, keepdims=True), count_send.shape[1:]
+        jnp.sum(flags_v[...].astype(F32), axis=1, keepdims=True), count_send.shape[1:]
     )
-    pl.semaphore_wait(barrier, len(peers))
-
-    for t in range(AHEAD):
-        wait_load(t)
-        own_ahead(t).start()
-        own_side(t).start()
 
     rows_at = lax.broadcasted_iota(jnp.int32, (HEAD_DIM, HEAD_DIM), 0)
     lanes_at = lax.broadcasted_iota(jnp.int32, (HEAD_DIM, HEAD_DIM), 1)
-    for m, seg in enumerate((seg_prev, seg_next)):
+    for m, seg in enumerate((seg_prev_v, seg_next_v)):
         def ids_at(index, seg=seg):
             return seg[:, pl.ds(pl.multiple_of(index * HEAD_DIM, HEAD_DIM), HEAD_DIM)].astype(F32)
 
@@ -166,6 +157,15 @@
                 block_bias = jnp.where(seq_at >= d, block_bias, -1e30)
             bias[m, d * HEAD_DIM : (d + 1) * HEAD_DIM, :] = block_bias
 
+    for t in range(AHEAD):
+        wait_load(t)
+    pl.semaphore_wait(barrier, len(peers))
+    for copy in counts_to(0):
+        copy.start()
+    for t in range(AHEAD):
+        own_ahead(t).start()
+        own_side(t).start()
+
     def window(w, which):
         return jnp.concatenate(
             [own[w, which], side[1 - core, w, which], near[w, which],
@@ -192,7 +192,7 @@
     def backward(w):
         k_all, v_all = window(w, 0), window(w, 1)
         k_turned = jnp.transpose(k_all)
-        flag_row = flags[...].astype(F32)
+        flag_row = flags_v[...].astype(F32)
         flag_pair = jnp.concatenate([flag_row, flag_row], axis=1)
         dk = dv = None
         for half in range(2):
@@ -259,6 +259,8 @@
     for copy in array_copies:
         copy.wait()
 
+    late = max(LAG + kv_heads // 2 + 7, COUNT_STEPS * rounds)
+
     def one_step(t, carry):
         @during(t, 0, chunks - AHEAD)
         def _():
@@ -286,23 +288,26 @@
             grads_side(t - LAG - 2).wait_recv()
             take_side(t - LAG - 2)
 
-        @during(t, LAG + 4, kv_heads)
-        def _():
-            far_back(t - LAG - 4).wait_recv()
-            take_far(t - LAG - 4)
-
-        for r in range(1, rounds + 1):
-            @pl.when(t == r)
+        @during(t, LAG + 5, kv_heads)
+        def _():
+            far_back(t - LAG - 5).wait_recv()
+            take_far(t - LAG - 5)
+
+        for r in range(rounds):
+            @pl.when(t == COUNT_STEPS * (r + 1) - 1)
             def _(r=r):
-                count_to(r - 1).wait_recv()
-                count_send[r] = count_send[r - 1] + count_recv[r - 1]
-
-        @during(t, LAG + 6, kv_heads)
-        def _():
-            near_back(t - LAG - 6).wait_recv()
-            take_near(t - LAG - 6)
-            gkv_copy(0, t - LAG - 6).start()
-            gkv_copy(1, t - LAG - 6).start()
+                total = count_send[r]
+                for j, copy in enumerate(counts_to(r)):
+                    copy.wait_recv()
+                    total = total + count_recv[r, j]
+                count_send[r + 1] = total
+
+        @during(t, late, kv_heads // 2)
+        def _():
+            for which in range(2):
+                w = 2 * (t - late) + which
+                near_back(w).wait_recv()
+                take_near(w)
 
         @during(t, LAG, chunks)
         def _():
@@ -318,29 +323,29 @@
         @during(t, LAG + kv_heads, kv_heads)
         def _():
             forward(t - LAG)
-            attn_copy(t - LAG - kv_heads).start()
-
-        @during(t, LAG + kv_heads, kv_heads)
-        def _():
-            finish_q(t - LAG - kv_heads)
-            gq_copy(t - LAG - kv_heads).start()
+
+        @during(t, late - 1, kv_heads // 2)
+        def _():
+            for which in range(2):
+                finish_q(2 * (t - late + 1) + which)
 
         @during(t, LAG + 2, kv_heads)
         def _():
             far_back(t - LAG - 2).start()
 
-        @during(t, LAG + 4, kv_heads)
-        def _():
-            near_back(t - LAG - 4).start()
-
-        for r in range(rounds):
-            @pl.when(t == r)
+        @during(t, LAG + 5, kv_heads)
+        def _():
+            near_back(t - LAG - 5).start()
+
+        for r in range(1, rounds):
+            @pl.when(t == COUNT_STEPS * r - 1)
             def _(r=r):
-                count_to(r).start()
+                for copy in counts_to(r):
+                    copy.start()
 
         return carry
 
-    steps = max(chunks + LAG, kv_heads + LAG + 6, rounds + 1)
+    steps = max(chunks + LAG, late + kv_heads // 2, COUNT_STEPS * rounds + 1)
     lax.fori_loop(0, steps, one_step, 0)
 
     def drain(t, carry):
@@ -357,15 +362,33 @@
         grads_side(g).wait_send()
         far_back(g).wait_send()
         near_back(g).wait_send()
-        attn_copy(g).wait()
-        gq_copy(g).wait()
-        gkv_copy(0, g).wait()
-        gkv_copy(1, g).wait()
         return carry
 
     lax.fori_loop(0, kv_heads, drain_back, 0)
     for r in range(rounds):
-        count_to(r).wait_send()
+        for copy in counts_to(r):
+            copy.wait_send()
+
+
+def write_out(*refs):
+    ins, outs, sems = refs[:4], refs[4:8], refs[8]
+    copies = [pltpu.make_async_copy(ins[i], outs[i], sems.at[i]) for i in range(4)]
+    for copy in copies:
+        copy.start()
+    for copy in copies:
+        copy.wait()
+
+
+def count_plan(n_fsdp, n_seq):
+    plan = []
+    for axis, size in (("seq", n_seq), ("fsdp", n_fsdp)):
+        stride = 1
+        while stride < size:
+            radix = min(8, size // stride)
+            plan.append((axis, stride, radix))
+            stride *= radix
+    first = plan.pop(0)
+    return [first] + plan[::-1]
 
 
 def body(n_fsdp, n_seq, *args):
@@ -374,23 +397,17 @@
     kv_heads = k.shape[1] // HEAD_DIM
     chunks = 2 * kv_heads
     width = q.shape[1]
-    rounds = int(math.log2(n_fsdp * n_seq))
+    plan = count_plan(n_fsdp, n_seq)
+    rounds, most = len(plan), max(radix for _, _, radix in plan) - 1
     tile = (2, HEAD_DIM, HEAD_DIM)
     anywhere = pl.BlockSpec(memory_space=pl.ANY)
     vmem = pl.BlockSpec(memory_space=pltpu.VMEM)
     dma = pltpu.SemaphoreType.DMA
-    return pl.pallas_call(
-        functools.partial(kernel, (kv_heads, n_fsdp, n_seq)),
-        out_shape=(
-            jax.ShapeDtypeStruct(q.shape, BF16),
-            jax.ShapeDtypeStruct(q.shape, BF16),
-            jax.ShapeDtypeStruct(k.shape, BF16),
-            jax.ShapeDtypeStruct(k.shape, BF16),
-        ),
-        in_specs=[
-            anywhere, anywhere, anywhere, vmem, anywhere, anywhere, anywhere, vmem, anywhere, vmem,
-        ],
-        out_specs=(anywhere,) * 4,
+    done = pl.pallas_call(
+        functools.partial(kernel, (kv_heads, n_fsdp, n_seq, plan)),
+        out_shape=tuple(pltpu.VMEM(x.shape, BF16) for x in (q, q, k, k)),
+        in_specs=[pl.BlockSpec(memory_space=pltpu.HBM)] * 10,
+        out_specs=(vmem,) * 4,
         scratch_shapes=[
             pltpu.VMEM((chunks,) + tile, BF16),
             pltpu.VMEM((chunks,) + tile, BF16),
@@ -406,28 +423,34 @@
             pltpu.VMEM((rows, width), BF16),
             pltpu.VMEM((rows, width), BF16),
             pltpu.VMEM((rows, width), BF16),
-            pltpu.VMEM((rows, width), BF16),
-            pltpu.VMEM((rows, width), BF16),
-            pltpu.VMEM(k.shape, BF16),
-            pltpu.VMEM(k.shape, BF16),
+            pltpu.VMEM(args[9].shape, jnp.int32),
+            pltpu.VMEM(args[7].shape, jnp.int32),
+            pltpu.VMEM(args[3].shape, jnp.int32),
             pltpu.VMEM((kv_heads, HEAD_DIM, GROUP * HEAD_DIM), F32),
             pltpu.VMEM((2, BLOCKS * HEAD_DIM, HEAD_DIM), F32),
             pltpu.VMEM((rounds + 1, 8, 128), F32),
-            pltpu.VMEM((rounds, 8, 128), F32),
+            pltpu.VMEM((rounds, most, 8, 128), F32),
             dma((chunks, 2)),
-            dma((3,)),
-            dma((4, kv_heads)),
+            dma((6,)),
             dma((5, chunks)),
             dma((5, chunks)),
             dma((3, kv_heads)),
             dma((3, kv_heads)),
-            dma((rounds,)),
-            dma((rounds,)),
+            dma((rounds, most)),
+            dma((rounds, most)),
         ],
         compiler_params=pltpu.CompilerParams(
             collective_id=0, has_side_effects=True, vmem_limit_bytes=60 * 1024 * 1024
         ),
     )(*args)
+    return pl.pallas_call(
+        write_out,
+        out_shape=tuple(jax.ShapeDtypeStruct(x.shape, BF16) for x in (q, q, k, k)),
+        in_specs=[anywhere] * 4,
+        out_specs=(anywhere,) * 4,
+        scratch_shapes=[dma((4,))],
+        compiler_params=pltpu.CompilerParams(vmem_limit_bytes=8 * 1024 * 1024),
+    )(*(pltpu.with_memory_space_constraint(x, pltpu.VMEM) for x in done))
 
 
 def solution(mesh):

time: 88.8 us -> 68.6 us (0.77)
  the two profiles are of different devices: /device:TPU:1 before, /device:TPU:9 now
where the time goes in v2:
time: 68.6 us; the launch traced here: 67.4 us
  Pallas kernels  66.8 us (97%)
    pallas_call x1, Pallas kernels, body(): pl.pallas_call(functools.partial(kernel, (kv_heads, n_fsdp, n_seq, plan))...  65.3 us
    pallas_call x1, Pallas kernels, body(): pl.pallas_call(write_out, out_shape=tuple((jax.ShapeDtypeStruct(x.shape,...  1.52 us

profile of v2, /device:TPU:9, one launch (start us, length us, event | category | flops | bytes accessed | tf_op | source)
XLA Modules:
  0.0 67.4 jit_solution(4245019683677334613)
XLA Ops:
  0.6 65.3 %shard_map.129 = (bf16[128,4096]{1,0:T(8,128)(2,1)S(1)}, bf16[128,4096]{1,0:T(8,128)(2,1)S(1)}, bf16[128,1024]{1,0:T(8,128)(2,1)S(1)}, bf16[128,1024]{1,0:T(8,128)(2,1)S(1)}) custom-call(bf16[128,4096]{1,0:T(8,128)(2,1)} %q_next.1, bf16[128,1024]{1,0:T(8,128)(2,1)} %k_next.1, bf16[128,1024]{1,0:T(8,128)(2,1)} %v_next.1, s32[1,4096]{1,0:T(1,128)} %seg_next.1, ...), custom_call_target="tpu_custom_call" | custom-call | tf_op jit(solution)/shard_map/pallas_call | solution.py:406
  65.9 1.5 %shard_map.130 = (bf16[128,4096]{1,0:T(8,128)(2,1)}, bf16[128,4096]{1,0:T(8,128)(2,1)}, bf16[128,1024]{1,0:T(8,128)(2,1)}, bf16[128,1024]{1,0:T(8,128)(2,1)}) custom-call(bf16[128,4096]{1,0:T(8,128)(2,1)S(1)} %get-tuple-element.8.refs_0_, bf16[128,4096]{1,0:T(8,128)(2,1)S(1)} %get-tuple-element.9.refs_1_, bf16[128,1024]{1,0:T(8,128)(2,1)S(1)} %get-tuple-element.10.refs_2_, ...), custom_call_target="tpu_custom_call" | custom-call | tf_op jit(solution)/shard_map/pallas_call | solution.py:446

commit v3 on v2

--- a/solution.py
+++ b/solution.py
@@ -12,7 +12,8 @@
 GROUP = 4
 BLOCKS = 5
 AHEAD = 2
-COUNT_STEPS = 5
+COUNT_STEPS = 4
+TURNS = 8
 LAG = 4
 MESH = pl.DeviceIdType.MESH
 F32 = jnp.float32
@@ -23,6 +24,11 @@
     return lax.dot_general(a, b, (dims, ((), ())), preferred_element_type=F32)
 
 
+def over_keys(values, join, reduce):
+    blocks = [values[d * HEAD_DIM : (d + 1) * HEAD_DIM] for d in range(BLOCKS)]
+    return reduce(functools.reduce(join, blocks), axis=0, keepdims=True)
+
+
 def column_of(row):
     return jnp.transpose(jnp.broadcast_to(row, (128, row.shape[1])))
 
@@ -31,9 +37,9 @@
     sizes,
     q_next, k_next, v_next, seg_next, q_prev, k_prev, v_prev, seg_prev, upstream, flags,
     attn_v, gq_v, gk_v, gv_v,
-    own, near, far, side, side_grads, side_recv, grads, far_send, far_recv, near_send, near_recv,
-    q_prev_v, up_v, q_next_v, flags_v, seg_prev_v, seg_next_v, dq_t, bias, count_send, count_recv,
-    load_sem, array_sem, send_sem, recv_sem, gsend_sem, grecv_sem, csend_sem, crecv_sem,
+    held, side, side_grads, side_recv, grads, far_send, far_recv, near_send, near_recv,
+    arrays_v, flags_v, seg_prev_v, seg_next_v, dq_t, bias, count_send, count_recv,
+    load_sem, small_sem, send_sem, recv_sem, gsend_sem, grecv_sem, csend_sem, crecv_sem,
 ):
     kv_heads, n_fsdp, n_seq, plan = sizes
     chunks = 2 * kv_heads
@@ -56,43 +62,44 @@
     ]
     rounds = len(plan)
 
-    def remote(src, dst, sems, at, device):
+    def remote(src, dst, sent, received, device):
         return pltpu.make_async_remote_copy(
-            src_ref=src, dst_ref=dst, send_sem=sems[0].at[at], recv_sem=sems[1].at[at],
+            src_ref=src, dst_ref=dst, send_sem=sent, recv_sem=received,
             device_id=device, device_id_type=MESH,
         )
 
-    links = (send_sem, recv_sem)
-    glinks = (gsend_sem, grecv_sem)
+    def pass_on(t, kind, src, dst, device):
+        return remote(
+            src, dst, send_sem.at[kind, t % TURNS], recv_sem.at[kind, t], {"seq": device}
+        )
 
     def own_ahead(t):
-        return remote(own.at[t], near.at[t], links, (0, t), {"seq": ahead_at})
+        return pass_on(t, 0, held.at[t, 0], held.at[t, 1], ahead_at)
 
     def near_ahead(t):
-        return remote(near.at[t], far.at[t], links, (1, t), {"seq": ahead_at})
-
-    def own_side(t):
-        return remote(own.at[t], side.at[0, t], links, (2, t), {"seq": side_at})
-
-    def near_side(t):
-        return remote(near.at[t], side.at[1, t], links, (3, t), {"seq": side_at})
-
-    def far_side(t):
-        return remote(far.at[t], side.at[2, t], links, (4, t), {"seq": side_at})
+        return pass_on(t, 1, held.at[t, 1], held.at[t, 2], ahead_at)
+
+    def all_side(t):
+        return pass_on(t, 2, held.at[t], side.at[t], side_at)
+
+    def give_back(t, kind, src, dst, device):
+        return remote(
+            src, dst, gsend_sem.at[kind, t % TURNS], grecv_sem.at[kind, t], {"seq": device}
+        )
 
     def grads_side(t):
-        return remote(side_grads.at[t], side_recv.at[t], glinks, (0, t), {"seq": side_at})
+        return give_back(t, 0, side_grads.at[t], side_recv.at[t], side_at)
 
     def far_back(t):
-        return remote(far_send.at[t], far_recv.at[t], glinks, (1, t), {"seq": behind_at})
+        return give_back(t, 1, far_send.at[t], far_recv.at[t], behind_at)
 
     def near_back(t):
-        return remote(near_send.at[t], near_recv.at[t], glinks, (2, t), {"seq": behind_at})
+        return give_back(t, 2, near_send.at[t], near_recv.at[t], behind_at)
 
     def counts_to(r):
         return [
             remote(
-                count_send.at[r], count_recv.at[r, j], (csend_sem, crecv_sem), (r, j), partner
+                count_send.at[r], count_recv.at[r, j], csend_sem.at[j], crecv_sem.at[r, j], partner
             )
             for j, partner in enumerate(partners[r])
         ]
@@ -101,13 +108,13 @@
         k_from, v_from = (k_prev, v_prev) if t < kv_heads else (k_next, v_next)
         src = (k_from, v_from)[which]
         columns = slice((t % kv_heads) * HEAD_DIM, (t % kv_heads + 1) * HEAD_DIM)
-        return pltpu.make_async_copy(src.at[:, columns], own.at[t, which], load_sem.at[t, which])
-
-    def wait_load(t):
-        for which, src in enumerate((k_prev, v_prev)):
-            pltpu.make_async_copy(
-                src.at[:, 0:HEAD_DIM], own.at[t, which], load_sem.at[t, which]
-            ).wait()
+        return pltpu.make_async_copy(
+            src.at[:, columns], held.at[t, 0, which], load_sem.at[int(t >= AHEAD)]
+        )
+
+    def wait_loads(first, last):
+        part = held.at[first:last, 0]
+        pltpu.make_async_copy(part, part, load_sem.at[int(first >= AHEAD)]).wait()
 
     def columns_of(g, count=GROUP):
         return pl.ds(pl.multiple_of(g * (count * HEAD_DIM), HEAD_DIM), count * HEAD_DIM)
@@ -117,21 +124,25 @@
     for peer in peers:
         pl.semaphore_signal(barrier, inc=1, device_id=peer, device_id_type=MESH)
 
+    for t in range(AHEAD):
+        load(t, 0).start()
+        load(t, 1).start()
     small = ((flags, flags_v), (seg_prev, seg_prev_v), (seg_next, seg_next_v))
     small_copies = [
-        pltpu.make_async_copy(src, dst, array_sem.at[3 + i]) for i, (src, dst) in enumerate(small)
+        pltpu.make_async_copy(src, dst, small_sem.at[i]) for i, (src, dst) in enumerate(small)
     ]
     for copy in small_copies:
         copy.start()
-    for t in range(chunks):
+    for t in range(AHEAD, chunks):
         load(t, 0).start()
         load(t, 1).start()
-    arrays = ((q_prev, q_prev_v), (upstream, up_v), (q_next, q_next_v))
-    array_copies = [
-        pltpu.make_async_copy(src, dst, array_sem.at[i]) for i, (src, dst) in enumerate(arrays)
-    ]
-    for copy in array_copies:
-        copy.start()
+    for i, src in enumerate((q_prev, upstream, q_next)):
+        pltpu.make_async_copy(src, arrays_v.at[i], load_sem.at[2]).start()
+
+    wait_loads(0, AHEAD)
+    pl.semaphore_wait(barrier, len(peers))
+    for t in range(AHEAD):
+        own_ahead(t).start()
 
     for copy in small_copies:
         copy.wait()
@@ -157,26 +168,22 @@
                 block_bias = jnp.where(seq_at >= d, block_bias, -1e30)
             bias[m, d * HEAD_DIM : (d + 1) * HEAD_DIM, :] = block_bias
 
-    for t in range(AHEAD):
-        wait_load(t)
-    pl.semaphore_wait(barrier, len(peers))
     for copy in counts_to(0):
         copy.start()
-    for t in range(AHEAD):
-        own_ahead(t).start()
-        own_side(t).start()
+    wait_loads(AHEAD, chunks)
+    pltpu.make_async_copy(arrays_v, arrays_v, load_sem.at[2]).wait()
 
     def window(w, which):
         return jnp.concatenate(
-            [own[w, which], side[1 - core, w, which], near[w, which],
-             side[2 - core, w, which], far[w, which]],
+            [held[w, 0, which], side[w, 1 - core, which], held[w, 1, which],
+             side[w, 2 - core, which], held[w, 2, which]],
             axis=0,
         )
 
-    def stacked(ref, g, first, count):
+    def stacked(i, g, first, count):
         return jnp.concatenate(
             [
-                ref[:, pl.ds(pl.multiple_of(g * width + j * HEAD_DIM, HEAD_DIM), HEAD_DIM)]
+                arrays_v[i, :, pl.ds(pl.multiple_of(g * width + j * HEAD_DIM, HEAD_DIM), HEAD_DIM)]
                 for j in range(first, first + count)
             ],
             axis=0,
@@ -185,9 +192,9 @@
     def expo(k_all, q_part, m):
         pair = bias[m]
         scores = dot(k_all, q_part, ((1,), (1,))) + jnp.concatenate([pair, pair], axis=1)
-        top = jnp.max(scores, axis=0, keepdims=True)
+        top = over_keys(scores, jnp.maximum, jnp.max)
         values = jnp.exp2((scores - top) * (scale * math.log2(math.e)))
-        return values, 1.0 / jnp.sum(values, axis=0, keepdims=True)
+        return values, 1.0 / over_keys(values, jnp.add, jnp.sum)
 
     def backward(w):
         k_all, v_all = window(w, 0), window(w, 1)
@@ -196,11 +203,11 @@
         flag_pair = jnp.concatenate([flag_row, flag_row], axis=1)
         dk = dv = None
         for half in range(2):
-            q_part = stacked(q_prev_v, w, 2 * half, 2)
-            u_part = stacked(up_v, w, 2 * half, 2)
+            q_part = stacked(0, w, 2 * half, 2)
+            u_part = stacked(1, w, 2 * half, 2)
             values, inverse = expo(k_all, q_part, 0)
             d_probs = dot(v_all, u_part, ((1,), (1,)))
-            row_delta = jnp.sum(values * d_probs, axis=0, keepdims=True) * inverse
+            row_delta = over_keys(values * d_probs, jnp.add, jnp.sum) * inverse
             probs = values * (inverse * flag_pair)
             d_scores = (probs * (d_probs - row_delta)).astype(BF16)
             dq_t[w, :, half * 256 : (half + 1) * 256] = dot(k_turned, d_scores, ((1,), (0,)))
@@ -218,15 +225,23 @@
 
     def forward(w):
         g = w - kv_heads
-        k_all, v_turned = window(w, 0), jnp.transpose(window(w, 1))
-        for half in range(2):
-            values, inverse = expo(k_all, stacked(q_next_v, g, 2 * half, 2), 1)
-            mixed = dot(v_turned, values.astype(BF16), ((1,), (0,))) * inverse
-            for j in range(2):
-                at = pl.multiple_of(g * width + (2 * half + j) * HEAD_DIM, HEAD_DIM)
-                attn_v[:, pl.ds(at, HEAD_DIM)] = jnp.transpose(
-                    mixed[:, j * HEAD_DIM : (j + 1) * HEAD_DIM]
-                ).astype(BF16)
+        k_all, v_all = window(w, 0), window(w, 1)
+        lower = jnp.concatenate([rows_at <= lanes_at] * GROUP, axis=1)
+        scores = dot(k_all, stacked(2, g, 0, GROUP), ((1,), (1,)))
+        scores = scores + jnp.concatenate([bias[1]] * GROUP, axis=1)
+        blocks = [scores[d * HEAD_DIM : (d + 1) * HEAD_DIM] for d in range(BLOCKS)]
+        blocks = [jnp.where(lower, blocks[0], blocks[4])] + blocks[1:4]
+        top = jnp.max(functools.reduce(jnp.maximum, blocks), axis=0, keepdims=True)
+        values = [jnp.exp2((x - top) * (scale * math.log2(math.e))) for x in blocks]
+        inverse = 1.0 / jnp.sum(functools.reduce(jnp.add, values), axis=0, keepdims=True)
+        ends = jnp.where(lower, values[0], 0.0), jnp.where(lower, 0.0, values[0])
+        parts = [x.astype(BF16) for x in [ends[0]] + values[1:] + [ends[1]]]
+        mixed = dot(jnp.transpose(v_all), jnp.concatenate(parts, axis=0), ((1,), (0,))) * inverse
+        for j in range(GROUP):
+            at = pl.multiple_of(g * width + j * HEAD_DIM, HEAD_DIM)
+            attn_v[:, pl.ds(at, HEAD_DIM)] = jnp.transpose(
+                mixed[:, j * HEAD_DIM : (j + 1) * HEAD_DIM]
+            ).astype(BF16)
 
     def factor_row():
         total = count_send[rounds, 0:1, :]
@@ -256,28 +271,22 @@
     def during(t, first, count):
         return pl.when((t >= first) & (t < first + count))
 
-    for copy in array_copies:
-        copy.wait()
-
-    late = max(LAG + kv_heads // 2 + 7, COUNT_STEPS * rounds)
+    late = max(LAG + kv_heads // 2 + 8, COUNT_STEPS * rounds + 3)
 
     def one_step(t, carry):
         @during(t, 0, chunks - AHEAD)
         def _():
-            wait_load(t + AHEAD)
             own_ahead(t + AHEAD).start()
-            own_side(t + AHEAD).start()
 
         @during(t, 0, chunks)
         def _():
             own_ahead(t).wait_recv()
             near_ahead(t).start()
-            near_side(t).start()
 
         @during(t, LAG - 1, chunks)
         def _():
             near_ahead(t - LAG + 1).wait_recv()
-            far_side(t - LAG + 1).start()
+            all_side(t - LAG + 1).start()
 
         @during(t, LAG + 1, kv_heads)
         def _():
@@ -298,36 +307,26 @@
             def _(r=r):
                 total = count_send[r]
                 for j, copy in enumerate(counts_to(r)):
-                    copy.wait_recv()
+                    copy.wait()
                     total = total + count_recv[r, j]
                 count_send[r + 1] = total
 
-        @during(t, late, kv_heads // 2)
+        @during(t, LAG, chunks)
+        def _():
+            all_side(t - LAG).wait_recv()
+
+        @during(t, LAG, kv_heads)
+        def _():
+            backward(t - LAG)
+
+        @during(t, LAG + kv_heads, kv_heads)
+        def _():
+            forward(t - LAG)
+
+        @during(t, late - 4, kv_heads // 2)
         def _():
             for which in range(2):
-                w = 2 * (t - late) + which
-                near_back(w).wait_recv()
-                take_near(w)
-
-        @during(t, LAG, chunks)
-        def _():
-            w = t - LAG
-            own_side(w).wait_recv()
-            near_side(w).wait_recv()
-            far_side(w).wait_recv()
-
-        @during(t, LAG, kv_heads)
-        def _():
-            backward(t - LAG)
-
-        @during(t, LAG + kv_heads, kv_heads)
-        def _():
-            forward(t - LAG)
-
-        @during(t, late - 1, kv_heads // 2)
-        def _():
-            for which in range(2):
-                finish_q(2 * (t - late + 1) + which)
+                finish_q(2 * (t - late + 4) + which)
 
         @during(t, LAG + 2, kv_heads)
         def _():
@@ -343,31 +342,29 @@
                 for copy in counts_to(r):
                     copy.start()
 
+        @during(t, late, kv_heads // 2)
+        def _():
+            for which in range(2):
+                w = 2 * (t - late) + which
+                near_back(w).wait_recv()
+                take_near(w)
+
+        @during(t, LAG, chunks)
+        def _():
+            own_ahead(t - LAG).wait_send()
+            near_ahead(t - LAG).wait_send()
+            all_side(t - LAG).wait_send()
+
+        @during(t, LAG + 8, kv_heads)
+        def _():
+            grads_side(t - LAG - 8).wait_send()
+            far_back(t - LAG - 8).wait_send()
+            near_back(t - LAG - 8).wait_send()
+
         return carry
 
-    steps = max(chunks + LAG, late + kv_heads // 2, COUNT_STEPS * rounds + 1)
+    steps = max(chunks + LAG, late + kv_heads // 2, kv_heads + LAG + 8, COUNT_STEPS * rounds + 1)
     lax.fori_loop(0, steps, one_step, 0)
-
-    def drain(t, carry):
-        own_ahead(t).wait_send()
-        near_ahead(t).wait_send()
-        own_side(t).wait_send()
-        near_side(t).wait_send()
-        far_side(t).wait_send()
-        return carry
-
-    lax.fori_loop(0, chunks, drain, 0)
-
-    def drain_back(g, carry):
-        grads_side(g).wait_send()
-        far_back(g).wait_send()
-        near_back(g).wait_send()
-        return carry
-
-    lax.fori_loop(0, kv_heads, drain_back, 0)
-    for r in range(rounds):
-        for copy in counts_to(r):
-            copy.wait_send()
 
 
 def write_out(*refs):
@@ -409,10 +406,8 @@
         in_specs=[pl.BlockSpec(memory_space=pltpu.HBM)] * 10,
         out_specs=(vmem,) * 4,
         scratch_shapes=[
-            pltpu.VMEM((chunks,) + tile, BF16),
-            pltpu.VMEM((chunks,) + tile, BF16),
-            pltpu.VMEM((chunks,) + tile, BF16),
-            pltpu.VMEM((3, chunks) + tile, BF16),
+            pltpu.VMEM((chunks, 3) + tile, BF16),
+            pltpu.VMEM((chunks, 3) + tile, BF16),
             pltpu.VMEM((kv_heads, 2) + tile, BF16),
             pltpu.VMEM((kv_heads, 2) + tile, BF16),
             pltpu.VMEM((kv_heads, 3) + tile, F32),
@@ -420,9 +415,7 @@
             pltpu.VMEM((kv_heads,) + tile, BF16),
             pltpu.VMEM((kv_heads,) + tile, BF16),
             pltpu.VMEM((kv_heads,) + tile, BF16),
-            pltpu.VMEM((rows, width), BF16),
-            pltpu.VMEM((rows, width), BF16),
-            pltpu.VMEM((rows, width), BF16),
+            pltpu.VMEM((3, rows, width), BF16),
             pltpu.VMEM(args[9].shape, jnp.int32),
             pltpu.VMEM(args[7].shape, jnp.int32),
             pltpu.VMEM(args[3].shape, jnp.int32),
@@ -430,13 +423,13 @@
             pltpu.VMEM((2, BLOCKS * HEAD_DIM, HEAD_DIM), F32),
             pltpu.VMEM((rounds + 1, 8, 128), F32),
             pltpu.VMEM((rounds, most, 8, 128), F32),
-            dma((chunks, 2)),
-            dma((6,)),
-            dma((5, chunks)),
-            dma((5, chunks)),
+            dma((3,)),
+            dma((3,)),
+            dma((3, TURNS)),
+            dma((3, chunks)),
+            dma((3, TURNS)),
             dma((3, kv_heads)),
-            dma((3, kv_heads)),
-            dma((rounds, most)),
+            dma((most,)),
             dma((rounds, most)),
         ],
         compiler_params=pltpu.CompilerParams(

time: 68.6 us -> 65.3 us (0.952)
  Pallas kernels: 66.8 us -> 63.5 us
    pallas_call x1, Pallas kernels: 65.3 us -> 62 us  [body(): pl.pallas_call(functools.partial(kernel, (kv_heads, n_fsdp, n_seq, plan))...]
where the time goes in v3:
time: 65.3 us; the launch traced here: 64.2 us
  Pallas kernels  63.5 us (97%)
    pallas_call x1, Pallas kernels, body(): pl.pallas_call(functools.partial(kernel, (kv_heads, n_fsdp, n_seq, plan))...  62 us
    pallas_call x1, Pallas kernels, body(): pl.pallas_call(write_out, out_shape=tuple((jax.ShapeDtypeStruct(x.shape,...  1.52 us

profile of v3, /device:TPU:9, one launch (start us, length us, event | category | flops | bytes accessed | tf_op | source)
XLA Modules:
  0.0 64.2 jit_solution(912801465564450250)
XLA Ops:
  0.6 62.0 %shard_map.129 = (bf16[128,4096]{1,0:T(8,128)(2,1)S(1)}, bf16[128,4096]{1,0:T(8,128)(2,1)S(1)}, bf16[128,1024]{1,0:T(8,128)(2,1)S(1)}, bf16[128,1024]{1,0:T(8,128)(2,1)S(1)}) custom-call(bf16[128,4096]{1,0:T(8,128)(2,1)} %q_next.1, bf16[128,1024]{1,0:T(8,128)(2,1)} %k_next.1, bf16[128,1024]{1,0:T(8,128)(2,1)} %v_next.1, s32[1,4096]{1,0:T(1,128)} %seg_next.1, ...), custom_call_target="tpu_custom_call" | custom-call | tf_op jit(solution)/shard_map/pallas_call | solution.py:403
  62.7 1.5 %shard_map.130 = (bf16[128,4096]{1,0:T(8,128)(2,1)}, bf16[128,4096]{1,0:T(8,128)(2,1)}, bf16[128,1024]{1,0:T(8,128)(2,1)}, bf16[128,1024]{1,0:T(8,128)(2,1)}) custom-call(bf16[128,4096]{1,0:T(8,128)(2,1)S(1)} %get-tuple-element.8.refs_0_, bf16[128,4096]{1,0:T(8,128)(2,1)S(1)} %get-tuple-element.9.refs_1_, bf16[128,1024]{1,0:T(8,128)(2,1)S(1)} %get-tuple-element.10.refs_2_, ...), custom_call_target="tpu_custom_call" | custom-call | tf_op jit(solution)/shard_map/pallas_call | solution.py:439

commit v4 on v3

--- a/solution.py
+++ b/solution.py
@@ -50,6 +50,8 @@
     ahead_at = (seq_at + 2) % n_seq
     behind_at = (seq_at + n_seq - 2) % n_seq
     side_at = seq_at + 1 - 2 * core
+    chip_at, last_chip = seq_at // 2, n_seq // 2 - 1
+    has_next, has_behind = chip_at < last_chip, chip_at > 0
     scale = HEAD_DIM ** -0.5
 
     partners = [
@@ -120,9 +122,17 @@
         return pl.ds(pl.multiple_of(g * (count * HEAD_DIM), HEAD_DIM), count * HEAD_DIM)
 
     barrier = pltpu.get_barrier_semaphore()
-    peers = [{"seq": ahead_at}, {"seq": behind_at}] + sum(partners, [])
+    peers = sum(partners, [])
     for peer in peers:
         pl.semaphore_signal(barrier, inc=1, device_id=peer, device_id_type=MESH)
+
+    @pl.when(has_next)
+    def _():
+        pl.semaphore_signal(barrier, inc=1, device_id={"seq": ahead_at}, device_id_type=MESH)
+
+    @pl.when(has_behind)
+    def _():
+        pl.semaphore_signal(barrier, inc=1, device_id={"seq": behind_at}, device_id_type=MESH)
 
     for t in range(AHEAD):
         load(t, 0).start()
@@ -139,10 +149,35 @@
     for i, src in enumerate((q_prev, upstream, q_next)):
         pltpu.make_async_copy(src, arrays_v.at[i], load_sem.at[2]).start()
 
+    def clear(ref, *at):
+        def one(t, carry):
+            ref[(t, *at)] = jnp.zeros(ref.shape[1 + len(at) :], ref.dtype)
+            return carry
+
+        lax.fori_loop(0, ref.shape[0], one, 0)
+
+    @pl.when(chip_at == 0)
+    def _():
+        clear(held, 1)
+        clear(far_recv)
+
+    @pl.when(chip_at <= 1)
+    def _():
+        clear(held, 2)
+
+    @pl.when(chip_at == last_chip)
+    def _():
+        clear(far_recv)
+        clear(near_recv)
+
     wait_loads(0, AHEAD)
-    pl.semaphore_wait(barrier, len(peers))
-    for t in range(AHEAD):
-        own_ahead(t).start()
+    ends = chip_at // last_chip + (last_chip - chip_at) // last_chip
+    pl.semaphore_wait(barrier, len(peers) + 2 - ends)
+
+    @pl.when(has_next)
+    def _():
+        for t in range(AHEAD):
+            own_ahead(t).start()
 
     for copy in small_copies:
         copy.wait()
@@ -268,24 +303,33 @@
         gk_v[:, columns_of(w, 1)] = (total[0] * (gain * scale)).astype(BF16)
         gv_v[:, columns_of(w, 1)] = (total[1] * gain).astype(BF16)
 
-    def during(t, first, count):
-        return pl.when((t >= first) & (t < first + count))
+    def during(t, first, count, also=None):
+        here = (t >= first) & (t < first + count)
+        return pl.when(here if also is None else here & also)
+
+    both_sides = has_next & has_behind
 
     late = max(LAG + kv_heads // 2 + 8, COUNT_STEPS * rounds + 3)
 
     def one_step(t, carry):
-        @during(t, 0, chunks - AHEAD)
+        @during(t, 0, chunks - AHEAD, has_next)
         def _():
             own_ahead(t + AHEAD).start()
 
-        @during(t, 0, chunks)
+        @during(t, 0, chunks, has_behind)
         def _():
             own_ahead(t).wait_recv()
+
+        @during(t, 0, chunks, both_sides)
+        def _():
             near_ahead(t).start()
 
+        @during(t, LAG - 1, chunks, chip_at > 1)
+        def _():
+            near_ahead(t - LAG + 1).wait_recv()
+
         @during(t, LAG - 1, chunks)
         def _():
-            near_ahead(t - LAG + 1).wait_recv()
             all_side(t - LAG + 1).start()
 
         @during(t, LAG + 1, kv_heads)
@@ -297,9 +341,12 @@
             grads_side(t - LAG - 2).wait_recv()
             take_side(t - LAG - 2)
 
+        @during(t, LAG + 5, kv_heads, both_sides)
+        def _():
+            far_back(t - LAG - 5).wait_recv()
+
         @during(t, LAG + 5, kv_heads)
         def _():
-            far_back(t - LAG - 5).wait_recv()
             take_far(t - LAG - 5)
 
         for r in range(rounds):
@@ -328,11 +375,11 @@
             for which in range(2):
                 finish_q(2 * (t - late + 4) + which)
 
-        @during(t, LAG + 2, kv_heads)
+        @during(t, LAG + 2, kv_heads, chip_at > 1)
         def _():
             far_back(t - LAG - 2).start()
 
-        @during(t, LAG + 5, kv_heads)
+        @during(t, LAG + 5, kv_heads, has_behind)
         def _():
             near_back(t - LAG - 5).start()
 
@@ -342,23 +389,38 @@
                 for copy in counts_to(r):
                     copy.start()
 
+        @during(t, late, kv_heads // 2, has_next)
+        def _():
+            for which in range(2):
+                near_back(2 * (t - late) + which).wait_recv()
+
         @during(t, late, kv_heads // 2)
         def _():
             for which in range(2):
-                w = 2 * (t - late) + which
-                near_back(w).wait_recv()
-                take_near(w)
+                take_near(2 * (t - late) + which)
+
+        @during(t, LAG, chunks, has_next)
+        def _():
+            own_ahead(t - LAG).wait_send()
+
+        @during(t, LAG, chunks, both_sides)
+        def _():
+            near_ahead(t - LAG).wait_send()
 
         @during(t, LAG, chunks)
         def _():
-            own_ahead(t - LAG).wait_send()
-            near_ahead(t - LAG).wait_send()
             all_side(t - LAG).wait_send()
 
         @during(t, LAG + 8, kv_heads)
         def _():
             grads_side(t - LAG - 8).wait_send()
+
+        @during(t, LAG + 8, kv_heads, chip_at > 1)
+        def _():
             far_back(t - LAG - 8).wait_send()
+
+        @during(t, LAG + 8, kv_heads, has_behind)
+        def _():
             near_back(t - LAG - 8).wait_send()
 
         return carry

time: 65.3 us -> 64.2 us (0.983); the launches traced: 64.2 us -> 64.2 us
  no operation moved by 1% of the time
where the time goes in v4:
time: 64.2 us
  Pallas kernels  63.5 us (99%)
    pallas_call x1, Pallas kernels, body(): pl.pallas_call(functools.partial(kernel, (kv_heads, n_fsdp, n_seq, plan))...  62 us
    pallas_call x1, Pallas kernels, body(): pl.pallas_call(write_out, out_shape=tuple((jax.ShapeDtypeStruct(x.shape,...  1.52 us

profile of v4, /device:TPU:9, one launch (start us, length us, event | category | flops | bytes accessed | tf_op | source)
XLA Modules:
  0.0 64.2 jit_solution(14265618672622266019)
XLA Ops:
  0.6 62.0 %shard_map.129 = (bf16[128,4096]{1,0:T(8,128)(2,1)S(1)}, bf16[128,4096]{1,0:T(8,128)(2,1)S(1)}, bf16[128,1024]{1,0:T(8,128)(2,1)S(1)}, bf16[128,1024]{1,0:T(8,128)(2,1)S(1)}) custom-call(bf16[128,4096]{1,0:T(8,128)(2,1)} %q_next.1, bf16[128,1024]{1,0:T(8,128)(2,1)} %k_next.1, bf16[128,1024]{1,0:T(8,128)(2,1)} %v_next.1, s32[1,4096]{1,0:T(1,128)} %seg_next.1, ...), custom_call_target="tpu_custom_call" | custom-call | tf_op jit(solution)/shard_map/pallas_call | solution.py:465
  62.6 1.5 %shard_map.130 = (bf16[128,4096]{1,0:T(8,128)(2,1)}, bf16[128,4096]{1,0:T(8,128)(2,1)}, bf16[128,1024]{1,0:T(8,128)(2,1)}, bf16[128,1024]{1,0:T(8,128)(2,1)}) custom-call(bf16[128,4096]{1,0:T(8,128)(2,1)S(1)} %get-tuple-element.8.refs_0_, bf16[128,4096]{1,0:T(8,128)(2,1)S(1)} %get-tuple-element.9.refs_1_, bf16[128,1024]{1,0:T(8,128)(2,1)S(1)} %get-tuple-element.10.refs_2_, ...), custom_call_target="tpu_custom_call" | custom-call | tf_op jit(solution)/shard_map/pallas_call | solution.py:501

commit v5 on v4

--- a/solution.py
+++ b/solution.py
@@ -12,7 +12,7 @@
 GROUP = 4
 BLOCKS = 5
 AHEAD = 2
-COUNT_STEPS = 4
+ROW_AT, TOTAL_AT = 8, 11
 TURNS = 8
 LAG = 4
 MESH = pl.DeviceIdType.MESH
@@ -38,10 +38,12 @@
     q_next, k_next, v_next, seg_next, q_prev, k_prev, v_prev, seg_prev, upstream, flags,
     attn_v, gq_v, gk_v, gv_v,
     held, side, side_grads, side_recv, grads, far_send, far_recv, near_send, near_recv,
-    arrays_v, flags_v, seg_prev_v, seg_next_v, dq_t, bias, count_send, count_recv,
-    load_sem, small_sem, send_sem, recv_sem, gsend_sem, grecv_sem, csend_sem, crecv_sem,
+    arrays_v, flags_v, seg_prev_v, seg_next_v, dq_t, bias,
+    count, row_counts, row_count, hub_counts, total_made, total_count,
+    load_sem, small_sem, send_sem, recv_sem, gsend_sem, grecv_sem,
+    count_sem, row_sem, across_sem, hub_sem, out_sem,
 ):
-    kv_heads, n_fsdp, n_seq, plan = sizes
+    kv_heads, n_fsdp, n_seq = sizes
     chunks = 2 * kv_heads
     width = GROUP * HEAD_DIM
     seq_at = lax.axis_index("seq")
@@ -54,15 +56,9 @@
     has_next, has_behind = chip_at < last_chip, chip_at > 0
     scale = HEAD_DIM ** -0.5
 
-    partners = [
-        [
-            {axis: at + ((at // stride % radix + j) % radix - at // stride % radix) * stride}
-            for j in range(1, radix)
-        ]
-        for axis, stride, radix in plan
-        for at in ((seq_at if axis == "seq" else fsdp_at),)
-    ]
-    rounds = len(plan)
+    is_hub = seq_at == 0
+    hub_one = (n_seq - seq_at) // n_seq
+    middle = n_seq // 4
 
     def remote(src, dst, sent, received, device):
         return pltpu.make_async_remote_copy(
@@ -98,13 +94,25 @@
     def near_back(t):
         return give_back(t, 2, near_send.at[t], near_recv.at[t], behind_at)
 
-    def counts_to(r):
-        return [
-            remote(
-                count_send.at[r], count_recv.at[r, j], csend_sem.at[j], crecv_sem.at[r, j], partner
-            )
-            for j, partner in enumerate(partners[r])
-        ]
+    def count_in():
+        return remote(count, row_counts.at[seq_at], count_sem.at[0], row_sem.at[seq_at], {"seq": 0})
+
+    def row_arrival(i):
+        return remote(count, row_counts.at[i], count_sem.at[0], row_sem.at[i], {"seq": 0})
+
+    def count_across(j):
+        return remote(
+            row_count, hub_counts.at[j], across_sem.at[j], hub_sem.at[j],
+            {"fsdp": (fsdp_at + j) % n_fsdp},
+        )
+
+    def count_out(i):
+        return remote(total_made, total_count, out_sem.at[i], count_sem.at[1], {"seq": i})
+
+    def count_behind():
+        return remote(
+            total_count, total_count, out_sem.at[0], count_sem.at[1], {"seq": behind_at}
+        )
 
     def load(t, which):
         k_from, v_from = (k_prev, v_prev) if t < kv_heads else (k_next, v_next)
@@ -122,9 +130,7 @@
         return pl.ds(pl.multiple_of(g * (count * HEAD_DIM), HEAD_DIM), count * HEAD_DIM)
 
     barrier = pltpu.get_barrier_semaphore()
-    peers = sum(partners, [])
-    for peer in peers:
-        pl.semaphore_signal(barrier, inc=1, device_id=peer, device_id_type=MESH)
+    pl.semaphore_signal(barrier, inc=1, device_id={"seq": side_at}, device_id_type=MESH)
 
     @pl.when(has_next)
     def _():
@@ -133,6 +139,18 @@
     @pl.when(has_behind)
     def _():
         pl.semaphore_signal(barrier, inc=1, device_id={"seq": behind_at}, device_id_type=MESH)
+
+    @pl.when(is_hub)
+    def _():
+        def one(i, carry):
+            pl.semaphore_signal(barrier, inc=1, device_id={"seq": i}, device_id_type=MESH)
+            return carry
+
+        lax.fori_loop(1, n_seq, one, 0)
+        for j in range(1, n_fsdp):
+            pl.semaphore_signal(
+                barrier, inc=1, device_id={"fsdp": (fsdp_at + j) % n_fsdp}, device_id_type=MESH
+            )
 
     for t in range(AHEAD):
         load(t, 0).start()
@@ -172,7 +190,7 @@
 
     wait_loads(0, AHEAD)
     ends = chip_at // last_chip + (last_chip - chip_at) // last_chip
-    pl.semaphore_wait(barrier, len(peers) + 2 - ends)
+    pl.semaphore_wait(barrier, 4 - ends + hub_one * (n_fsdp - 2))
 
     @pl.when(has_next)
     def _():
@@ -181,8 +199,8 @@
 
     for copy in small_copies:
         copy.wait()
-    count_send[0] = jnp.broadcast_to(
-        jnp.sum(flags_v[...].astype(F32), axis=1, keepdims=True), count_send.shape[1:]
+    count[...] = jnp.broadcast_to(
+        jnp.sum(flags_v[...].astype(F32), axis=1, keepdims=True), count.shape
     )
 
     rows_at = lax.broadcasted_iota(jnp.int32, (HEAD_DIM, HEAD_DIM), 0)
@@ -203,8 +221,10 @@
                 block_bias = jnp.where(seq_at >= d, block_bias, -1e30)
             bias[m, d * HEAD_DIM : (d + 1) * HEAD_DIM, :] = block_bias
 
-    for copy in counts_to(0):
-        copy.start()
+    @pl.when(seq_at > 0)
+    def _():
+        count_in().start()
+
     wait_loads(AHEAD, chunks)
     pltpu.make_async_copy(arrays_v, arrays_v, load_sem.at[2]).wait()
 
@@ -279,7 +299,7 @@
             ).astype(BF16)
 
     def factor_row():
-        total = count_send[rounds, 0:1, :]
+        total = total_count[0:1, :]
         return (HEAD_DIM * n_fsdp * n_seq) / jnp.maximum(total, 1.0)
 
     def finish_q(g):
@@ -309,7 +329,7 @@
 
     both_sides = has_next & has_behind
 
-    late = max(LAG + kv_heads // 2 + 8, COUNT_STEPS * rounds + 3)
+    late = max(LAG + kv_heads // 2 + 8, TOTAL_AT + 5)
 
     def one_step(t, carry):
         @during(t, 0, chunks - AHEAD, has_next)
@@ -349,14 +369,32 @@
         def _():
             take_far(t - LAG - 5)
 
-        for r in range(rounds):
-            @pl.when(t == COUNT_STEPS * (r + 1) - 1)
-            def _(r=r):
-                total = count_send[r]
-                for j, copy in enumerate(counts_to(r)):
-                    copy.wait()
-                    total = total + count_recv[r, j]
-                count_send[r + 1] = total
+        @pl.when((t == ROW_AT) & is_hub)
+        def _():
+            def one(i, total):
+                row_arrival(i).wait_recv()
+                return total + row_counts[i]
+
+            row_count[...] = lax.fori_loop(1, n_seq, one, count[...])
+
+        @pl.when((t == TOTAL_AT) & is_hub)
+        def _():
+            total = row_count[...]
+            for j in range(1, n_fsdp):
+                count_across(j).wait()
+                total = total + hub_counts[j]
+            total_made[...] = total
+            total_count[...] = total
+
+        @pl.when((t == TOTAL_AT) & (seq_at > 0) & (chip_at != middle))
+        def _():
+            count_out(0).wait_recv()
+            count_in().wait_send()
+
+        @pl.when((t == TOTAL_AT + 1) & (chip_at == middle))
+        def _():
+            count_behind().wait_recv()
+            count_in().wait_send()
 
         @during(t, LAG, chunks)
         def _():
@@ -383,11 +421,36 @@
         def _():
             near_back(t - LAG - 5).start()
 
-        for r in range(1, rounds):
-            @pl.when(t == COUNT_STEPS * r - 1)
-            def _(r=r):
-                for copy in counts_to(r):
-                    copy.start()
+        @pl.when((t == ROW_AT) & is_hub)
+        def _():
+            for j in range(1, n_fsdp):
+                count_across(j).start()
+
+        @pl.when((t == TOTAL_AT) & is_hub)
+        def _():
+            def one(i, carry):
+                count_out(i).start()
+                return carry
+
+            lax.fori_loop(1, 2 * middle, one, 0)
+            lax.fori_loop(2 * middle + 2, n_seq, one, 0)
+
+        @pl.when((t == TOTAL_AT) & (chip_at == middle + 1))
+        def _():
+            count_behind().start()
+
+        @pl.when((t == TOTAL_AT + 2) & (chip_at == middle + 1))
+        def _():
+            count_behind().wait_send()
+
+        @pl.when((t == TOTAL_AT + 2) & is_hub)
+        def _():
+            def one(i, carry):
+                count_out(i).wait_send()
+                return carry
+
+            lax.fori_loop(1, 2 * middle, one, 0)
+            lax.fori_loop(2 * middle + 2, n_seq, one, 0)
 
         @during(t, late, kv_heads // 2, has_next)
         def _():
@@ -425,7 +488,7 @@
 
         return carry
 
-    steps = max(chunks + LAG, late + kv_heads // 2, kv_heads + LAG + 8, COUNT_STEPS * rounds + 1)
+    steps = max(chunks + LAG, late + kv_heads // 2, kv_heads + LAG + 8, TOTAL_AT + 3)
     lax.fori_loop(0, steps, one_step, 0)
 
 
@@ -438,32 +501,18 @@
         copy.wait()
 
 
-def count_plan(n_fsdp, n_seq):
-    plan = []
-    for axis, size in (("seq", n_seq), ("fsdp", n_fsdp)):
-        stride = 1
-        while stride < size:
-            radix = min(8, size // stride)
-            plan.append((axis, stride, radix))
-            stride *= radix
-    first = plan.pop(0)
-    return [first] + plan[::-1]
-
-
 def body(n_fsdp, n_seq, *args):
     q, k = args[0], args[1]
     rows = q.shape[0]
     kv_heads = k.shape[1] // HEAD_DIM
     chunks = 2 * kv_heads
     width = q.shape[1]
-    plan = count_plan(n_fsdp, n_seq)
-    rounds, most = len(plan), max(radix for _, _, radix in plan) - 1
     tile = (2, HEAD_DIM, HEAD_DIM)
     anywhere = pl.BlockSpec(memory_space=pl.ANY)
     vmem = pl.BlockSpec(memory_space=pltpu.VMEM)
     dma = pltpu.SemaphoreType.DMA
     done = pl.pallas_call(
-        functools.partial(kernel, (kv_heads, n_fsdp, n_seq, plan)),
+        functools.partial(kernel, (kv_heads, n_fsdp, n_seq)),
         out_shape=tuple(pltpu.VMEM(x.shape, BF16) for x in (q, q, k, k)),
         in_specs=[pl.BlockSpec(memory_space=pltpu.HBM)] * 10,
         out_specs=(vmem,) * 4,
@@ -483,16 +532,23 @@
             pltpu.VMEM(args[3].shape, jnp.int32),
             pltpu.VMEM((kv_heads, HEAD_DIM, GROUP * HEAD_DIM), F32),
             pltpu.VMEM((2, BLOCKS * HEAD_DIM, HEAD_DIM), F32),
-            pltpu.VMEM((rounds + 1, 8, 128), F32),
-            pltpu.VMEM((rounds, most, 8, 128), F32),
+            pltpu.VMEM((8, 128), F32),
+            pltpu.VMEM((n_seq, 8, 128), F32),
+            pltpu.VMEM((8, 128), F32),
+            pltpu.VMEM((n_fsdp, 8, 128), F32),
+            pltpu.VMEM((8, 128), F32),
+            pltpu.VMEM((8, 128), F32),
             dma((3,)),
             dma((3,)),
             dma((3, TURNS)),
             dma((3, chunks)),
             dma((3, TURNS)),
             dma((3, kv_heads)),
-            dma((most,)),
-            dma((rounds, most)),
+            dma((2,)),
+            dma((n_seq,)),
+            dma((n_fsdp,)),
+            dma((n_fsdp,)),
+            dma((n_seq,)),
         ],
         compiler_params=pltpu.CompilerParams(
             collective_id=0, has_side_effects=True, vmem_limit_bytes=60 * 1024 * 1024

time: 64.2 us -> 60.1 us (0.936)
  Pallas kernels: 63.5 us -> 59.1 us
    pallas_call x1, Pallas kernels: 62 us -> 57.6 us  [body(): pl.pallas_call(functools.partial(kernel, (kv_heads, n_fsdp, n_seq)), out_...]
where the time goes in v5:
time: 60.1 us; the launch traced here: 59.7 us
  Pallas kernels  59.1 us (98%)
  between operations  0.64 us (1%)
    pallas_call x1, Pallas kernels, body(): pl.pallas_call(functools.partial(kernel, (kv_heads, n_fsdp, n_seq)), out_...  57.6 us
    pallas_call x1, Pallas kernels, body(): pl.pallas_call(write_out, out_shape=tuple((jax.ShapeDtypeStruct(x.shape,...  1.52 us

profile of v5, /device:TPU:9, one launch (start us, length us, event | category | flops | bytes accessed | tf_op | source)
XLA Modules:
  0.0 59.7 jit_solution(2081663817612341249)
XLA Ops:
  0.6 57.6 %shard_map.129 = (bf16[128,4096]{1,0:T(8,128)(2,1)S(1)}, bf16[128,4096]{1,0:T(8,128)(2,1)S(1)}, bf16[128,1024]{1,0:T(8,128)(2,1)S(1)}, bf16[128,1024]{1,0:T(8,128)(2,1)S(1)}) custom-call(bf16[128,4096]{1,0:T(8,128)(2,1)} %q_next.1, bf16[128,1024]{1,0:T(8,128)(2,1)} %k_next.1, bf16[128,1024]{1,0:T(8,128)(2,1)} %v_next.1, s32[1,4096]{1,0:T(1,128)} %seg_next.1, ...), custom_call_target="tpu_custom_call" | custom-call | tf_op jit(solution)/shard_map/pallas_call | solution.py:514
  58.2 1.5 %shard_map.130 = (bf16[128,4096]{1,0:T(8,128)(2,1)}, bf16[128,4096]{1,0:T(8,128)(2,1)}, bf16[128,1024]{1,0:T(8,128)(2,1)}, bf16[128,1024]{1,0:T(8,128)(2,1)}) custom-call(bf16[128,4096]{1,0:T(8,128)(2,1)S(1)} %get-tuple-element.8.refs_0_, bf16[128,4096]{1,0:T(8,128)(2,1)S(1)} %get-tuple-element.9.refs_1_, bf16[128,1024]{1,0:T(8,128)(2,1)S(1)} %get-tuple-element.10.refs_2_, ...), custom_call_target="tpu_custom_call" | custom-call | tf_op jit(solution)/shard_map/pallas_call | solution.py:557

commit v6 on v5

--- a/solution.py
+++ b/solution.py
@@ -14,6 +14,7 @@
 AHEAD = 2
 ROW_AT, TOTAL_AT = 8, 11
 TURNS = 8
+BACK_TURNS = 4
 LAG = 4
 MESH = pl.DeviceIdType.MESH
 F32 = jnp.float32
@@ -82,7 +83,7 @@
 
     def give_back(t, kind, src, dst, device):
         return remote(
-            src, dst, gsend_sem.at[kind, t % TURNS], grecv_sem.at[kind, t], {"seq": device}
+            src, dst, gsend_sem.at[kind, t % BACK_TURNS], grecv_sem.at[kind, t], {"seq": device}
         )
 
     def grads_side(t):
@@ -474,13 +475,13 @@
         def _():
             all_side(t - LAG).wait_send()
 
-        @during(t, LAG + 8, kv_heads)
-        def _():
-            grads_side(t - LAG - 8).wait_send()
-
-        @during(t, LAG + 8, kv_heads, chip_at > 1)
-        def _():
-            far_back(t - LAG - 8).wait_send()
+        @during(t, LAG + 4, kv_heads)
+        def _():
+            grads_side(t - LAG - 4).wait_send()
+
+        @during(t, LAG + 5, kv_heads, chip_at > 1)
+        def _():
+            far_back(t - LAG - 5).wait_send()
 
         @during(t, LAG + 8, kv_heads, has_behind)
         def _():
@@ -542,7 +543,7 @@
             dma((3,)),
             dma((3, TURNS)),
             dma((3, chunks)),
-            dma((3, TURNS)),
+            dma((3, BACK_TURNS)),
             dma((3, kv_heads)),
             dma((2,)),
             dma((n_seq,)),

time: 60.1 us -> 60 us (level)
  no operation moved by 1% of the time
where the time goes in v6:
time: 60 us; the launch traced here: 59.6 us
  Pallas kernels  59 us (98%)
  between operations  0.64 us (1%)
    pallas_call x1, Pallas kernels, body(): pl.pallas_call(functools.partial(kernel, (kv_heads, n_fsdp, n_seq)), out_...  57.5 us
    pallas_call x1, Pallas kernels, body(): pl.pallas_call(write_out, out_shape=tuple((jax.ShapeDtypeStruct(x.shape,...  1.52 us

profile of v6, /device:TPU:9, one launch (start us, length us, event | category | flops | bytes accessed | tf_op | source)
XLA Modules:
  0.0 59.6 jit_solution(7535117271228649666)
XLA Ops:
  0.6 57.5 %shard_map.129 = (bf16[128,4096]{1,0:T(8,128)(2,1)S(1)}, bf16[128,4096]{1,0:T(8,128)(2,1)S(1)}, bf16[128,1024]{1,0:T(8,128)(2,1)S(1)}, bf16[128,1024]{1,0:T(8,128)(2,1)S(1)}) custom-call(bf16[128,4096]{1,0:T(8,128)(2,1)} %q_next.1, bf16[128,1024]{1,0:T(8,128)(2,1)} %k_next.1, bf16[128,1024]{1,0:T(8,128)(2,1)} %v_next.1, s32[1,4096]{1,0:T(1,128)} %seg_next.1, ...), custom_call_target="tpu_custom_call" | custom-call | tf_op jit(solution)/shard_map/pallas_call | solution.py:515
  58.1 1.5 %shard_map.130 = (bf16[128,4096]{1,0:T(8,128)(2,1)}, bf16[128,4096]{1,0:T(8,128)(2,1)}, bf16[128,1024]{1,0:T(8,128)(2,1)}, bf16[128,1024]{1,0:T(8,128)(2,1)}) custom-call(bf16[128,4096]{1,0:T(8,128)(2,1)S(1)} %get-tuple-element.8.refs_0_, bf16[128,4096]{1,0:T(8,128)(2,1)S(1)} %get-tuple-element.9.refs_1_, bf16[128,1024]{1,0:T(8,128)(2,1)S(1)} %get-tuple-element.10.refs_2_, ...), custom_call_target="tpu_custom_call" | custom-call | tf_op jit(solution)/shard_map/pallas_call | solution.py:558
